TPU v7x, 32 devices: a whole 2x2x4 slice. The times are simulated.
32 devices in a mesh: ka: 16 (over z, y, core), ga: 2 (over x).
Axes of the slice: x: 2, y: 2, z: 4, core: 2. Of those that a mesh axis runs over, the one named last changes fastest.
Arguments:
- coeffs: bfloat16 [16, 240, 2, 64, 128], P('ka', 'ga'), may hold values from -0.44921875 to 0.44921875
- neighbour: int32 [16, 3], P('ka'), may hold values from 0 to 15, as said below
- shift_id: int32 [16, 3], P('ka'), may hold values from 0 to 7
- block_map: int32 [8, 240], replicated, may hold values from 0 to 239, as said below
Outputs:
- intersection: float32 [16, 3, 2, 64, 64], P('ka', None, None, 'ga')
Inputs may be any that keep to these rules, and one draw needn't show every extreme that they name: `neighbour`: the k-points are numbered helically. The three columns of row k hold (k + 1) mod 16, (k + 4) mod 16 and (k + 8) mod 16, in an order drawn for each row. `block_map`: each row is a permutation of the 240 blocks. Block j lies in G-slice j // 120. In every row, each G-slice receives exactly 20 of its blocks from one other G-slice, exactly 10 from each of the remaining other G-slices, and the rest from itself.
All inputs are finite; a program needn't handle non-finite values.
Results may differ from a plain program's by a relative error of at most 0.0003.
Values may be sent and summed in bfloat16 or wider, within the bound.
A program may use at most 128 MiB of HBM per device.

v0:
```python
import jax
import jax.numpy as jnp
from jax import lax
from jax.sharding import PartitionSpec as P


def shifted(block, axis, distance):
    devices = range(lax.axis_size(axis))
    route = [((i - distance) % len(devices), i) for i in devices]
    return lax.ppermute(block, axis, route)


def complex_intersection(bra_real, bra_imag, ket_real, ket_imag, form):
    real_part = jnp.einsum(form, bra_real, ket_real, preferred_element_type=jnp.float32)
    real_part = real_part + jnp.einsum(form, bra_imag, ket_imag, preferred_element_type=jnp.float32)
    imag_part = jnp.einsum(form, bra_real, ket_imag, preferred_element_type=jnp.float32)
    imag_part = imag_part - jnp.einsum(form, bra_imag, ket_real, preferred_element_type=jnp.float32)
    return jnp.stack([real_part, imag_part], axis=-3)


def slot_plan(
    home_slice, target_slice, sent_local, place_local, my_slice, slices, capacity, slab_blocks
):
    targets = jnp.arange(slices, dtype=jnp.int32)
    chosen = (home_slice == my_slice)[:, None, :] & (
        target_slice[:, None, :] == targets[None, :, None]
    )
    chosen = chosen & (targets != my_slice)[None, :, None]
    counted = jnp.cumsum(chosen.astype(jnp.int32), axis=2) - 1
    places = jnp.arange(capacity, dtype=jnp.int32)
    matched = (
        chosen[:, :, None, :] & (counted[:, :, None, :] == places[None, None, :, None])
    ).astype(jnp.int32)
    filled = jnp.sum(matched, axis=3)
    sent_block = jnp.sum(matched * sent_local[:, None, None, :], axis=3)
    where_to = jnp.sum(matched * place_local[:, None, None, :], axis=3) + (1 - filled) * slab_blocks
    pair_count = home_slice.shape[0]
    return (
        sent_block.reshape(pair_count, slices * capacity),
        where_to.reshape(pair_count, slices * capacity),
    )


def on_device(coeffs, neighbour, shift_id, block_map):
    k_local = coeffs.shape[0]
    slab_blocks = coeffs.shape[1]
    band_count = coeffs.shape[3]
    lane_width = coeffs.shape[4]
    vector_count = neighbour.shape[1]
    cycle_size = lax.axis_size("ka")
    slices = lax.axis_size("ga")
    my_cycle = lax.axis_index("ka")
    my_slice = lax.axis_index("ga")
    capacity = 2 * max(1, slab_blocks // 12)
    all_blocks = slab_blocks * slices
    pair_count = k_local * vector_count
    k_total = k_local * cycle_size
    row_points = min(16, k_total // 4)
    row_devices = row_points // k_local
    pad_spec = ((0, 0), (0, 1), (0, 0), (0, 0), (0, 0))
    row_point = shifted(coeffs, "ka", -1)
    row_source = jnp.mod(my_cycle + 1, cycle_size)
    plane_kets = shifted(coeffs, "ka", -row_devices)
    plane_source = jnp.mod(my_cycle + row_devices, cycle_size)
    opposite = shifted(coeffs, "ka", cycle_size // 2)
    targets_flat = neighbour.reshape(-1)
    shifts_flat = shift_id.reshape(-1)
    target_device = targets_flat // k_local
    target_lane = targets_flat - target_device * k_local
    ket_index = jnp.where(
        target_device == my_cycle,
        target_lane,
        jnp.where(
            target_device == row_source,
            k_local,
            jnp.where(
                target_device == plane_source,
                k_local + 1 + target_lane,
                2 * k_local + 1 + target_lane,
            ),
        ),
    )
    bra_index = jnp.arange(pair_count, dtype=jnp.int32) // vector_count
    picks = (
        shifts_flat[:, None] == jnp.arange(block_map.shape[0], dtype=jnp.int32)[None, :]
    ).astype(jnp.int32)
    relabel = jnp.sum(picks[:, :, None] * block_map[None, :, :], axis=1)
    dest_global = jnp.broadcast_to(jnp.arange(all_blocks, dtype=jnp.int32)[None, :], relabel.shape)
    source_slice = relabel // slab_blocks
    dest_slice = dest_global // slab_blocks
    source_local = relabel - source_slice * slab_blocks
    dest_local = dest_global - dest_slice * slab_blocks
    kets = jnp.pad(jnp.concatenate([coeffs, row_point, plane_kets, opposite], axis=0), pad_spec)
    own_source = lax.dynamic_slice_in_dim(relabel, my_slice * slab_blocks, slab_blocks, 1)
    self_place = jnp.where(
        own_source // slab_blocks == my_slice, own_source - my_slice * slab_blocks, slab_blocks
    )
    ket_self = kets[ket_index[:, None], self_place]
    ket_self = ket_self.reshape(k_local, vector_count, slab_blocks, 2, band_count, lane_width)
    local_terms = complex_intersection(
        coeffs[:, :, 0],
        coeffs[:, :, 1],
        ket_self[:, :, :, 0],
        ket_self[:, :, :, 1],
        "ksmw,kbsnw->kbmn",
    )
    sent_block, where_to = slot_plan(
        dest_slice, source_slice, dest_local, source_local, my_slice, slices, capacity, slab_blocks
    )
    payload = coeffs[bra_index[:, None], sent_block]
    owner = jnp.broadcast_to(ket_index[:, None], (pair_count, slices))
    blocks = lax.all_to_all(payload, "ga", split_axis=1, concat_axis=1, tiled=True)
    places_in = lax.all_to_all(where_to, "ga", split_axis=1, concat_axis=1, tiled=True)
    owners = lax.all_to_all(owner, "ga", split_axis=1, concat_axis=1, tiled=True)
    partner = kets[owners[:, 0][:, None], places_in]
    remote = complex_intersection(
        blocks[:, :, 0], blocks[:, :, 1], partner[:, :, 0], partner[:, :, 1], "ismw,isnw->imn"
    )
    summed_part = local_terms + remote.reshape(k_local, vector_count, 2, band_count, band_count)
    total = lax.psum(summed_part, "ga")
    row_count = band_count // slices
    return lax.dynamic_slice_in_dim(total, my_slice * row_count, row_count, 3)


def solution(mesh):
    in_specs = (P("ka", "ga", None, None, None), P("ka", None), P("ka", None), P())
    out_specs = P("ka", None, None, "ga", None)
    return jax.shard_map(
        on_device, mesh=mesh, in_specs=in_specs, out_specs=out_specs, check_vma=False
    )
```

profile of v0, /device:TPU:0, one launch (start us, length us, event | category | flops | bytes accessed | tf_op | source)
XLA Modules:
  0.0 407.5 jit_solution(8698845887954236146)
XLA Ops:
  6.5 5.5 %collective-permute-start = (bf16[1,120,2,64,128]{4,3,2,1,0:T(8,128)(2,1)}, bf16[1,120,2,64,128]{4,3,2,1,0:T(8,128)(2,1)}, u32[]{:S(2)}, u32[]{:S(2)}) collective-permute-start(bf16[1,120,2,64,128]{4,3,2,1,0:T(8,128)(2,1)} %param.4), channel_id=1, source_target_pairs={{2,0},{4,2},{6,4},{8,6},{10,8},{12,10},{14,12},{16,14},{18,16},{20... | collective-permute-start | bytes 11796488 | tf_op jit(solution)/shard_map/ppermute | solution.py:10
  12.0 0.4 collective-permute-start.1
  12.5 0.0 collective-permute-start.2
  12.5 0.7 clamp_shift-left_fusion
  13.1 0.6 broadcast_in_dim.35
  13.7 3.2 all-to-all-start.1
  16.9 0.7 fusion.68
  17.6 0.8 multiply_reduce_fusion
  18.4 0.1 and_and_fusion
  18.6 1.8 reduce-window.6
  20.4 0.1 slice.56
  20.5 0.1 copy.78
  20.6 0.1 copy.79
  20.7 0.1 broadcast_add_fusion
  20.8 3.1 select_reduce_fusion.1
  24.0 0.1 copy.83
  24.1 0.1 copy.84
  24.2 0.6 copy.85
  24.8 0.1 copy.80
  24.9 0.1 reshape.387
  25.0 0.1 fusion.63
  25.0 0.0 all-to-all-done.1
  25.0 3.3 all-to-all-start.2
  28.3 0.1 reshape.395
  28.4 5.1 %gather_fusion.1 = bf16[120,2,64,128]{3,2,1,0:T(8,128)(2,1)} fusion(bf16[1,120,2,64,128]{4,3,2,1,0:T(8,128)(2,1)} %param.4, s32[120]{0:T(128)S(1)} %reshape.395), kind=kCustom, calls=%fused_computation.1 | custom fusion | bytes 7865280 | tf_op jit(solution)/shard_map/gather | solution.py:110
  33.5 5.4 %copy.81 = bf16[3,40,2,64,128]{4,3,0,2,1:T(8,128)(2,1)} copy(bf16[3,40,2,64,128]{4,3,2,1,0:T(8,128)(2,1)} %bitcast.179) | data formatting | bytes 7864320 | tf_op jit(solution)/shard_map/gather | solution.py:110
  38.9 0.0 all-to-all-done.2
  38.9 5.5 %all-to-all-start = ((bf16[3,40,2,64,128]{4,3,0,2,1:T(8,128)(2,1)}), bf16[3,40,2,64,128]{4,3,0,2,1:T(8,128)(2,1)}, u32[]{:S(2)}, u32[]{:S(2)}) async-start(bf16[3,40,2,64,128]{4,3,0,2,1:T(8,128)(2,1)} %copy.81), calls=%async_computation | async-start | bytes 7864320 | tf_op jit(solution)/shard_map/all_to_all | solution.py:112
  44.4 0.2 all-reduce.4.cloned.1.call-start
  44.6 0.1 fusion.60
  44.7 0.1 reshape.389
  44.8 0.1 all_to_all.19
  44.9 0.1 fusion.66
  44.9 0.1 reshape.401
  45.0 43.7 %all-to-all-done = bf16[3,40,2,64,128]{4,3,0,2,1:T(8,128)(2,1)} async-done(((bf16[3,40,2,64,128]{4,3,0,2,1:T(8,128)(2,1)}), bf16[3,40,2,64,128]{4,3,0,2,1:T(8,128)(2,1)}, u32[]{:S(2)}, u32[]{:S(2)}) %all-to-all-start) | async-done | bytes 3932192 | tf_op jit(solution)/shard_map/all_to_all | solution.py:112
  88.7 4.5 %fusion.77 = (bf16[3,40,1,64,128]{4,3,0,2,1:T(8,128)(2,1)S(1)}, bf16[3,40,1,64,128]{4,3,0,2,1:T(8,128)(2,1)}) fusion(bf16[3,40,2,64,128]{4,3,0,2,1:T(8,128)(2,1)} %all-to-all-done), kind=kLoop, calls=%fused_computation.110 | loop fusion | bytes 7864320 | tf_op jit(solution)/shard_map/slice | solution.py:117
  93.2 4.5 %collective-permute-done = bf16[1,120,2,64,128]{4,3,2,1,0:T(8,128)(2,1)} collective-permute-done((bf16[1,120,2,64,128]{4,3,2,1,0:T(8,128)(2,1)}, bf16[1,120,2,64,128]{4,3,2,1,0:T(8,128)(2,1)}, u32[]{:S(2)}, u32[]{:S(2)}) %collective-permute-start) | collective-permute-done | bytes 3932192 | tf_op jit(solution)/shard_map/ppermute | solution.py:10
  97.7 83.4 %collective-permute-done.1 = bf16[1,120,2,64,128]{4,3,2,1,0:T(8,128)(2,1)} collective-permute-done((bf16[1,120,2,64,128]{4,3,2,1,0:T(8,128)(2,1)}, bf16[1,120,2,64,128]{4,3,2,1,0:T(8,128)(2,1)}, u32[]{:S(2)}, u32[]{:S(2)}) %collective-permute-start.1) | collective-permute-done | bytes 3932192 | tf_op jit(solution)/shard_map/ppermute | solution.py:10
  181.1 126.2 %collective-permute-done.2 = bf16[1,120,2,64,128]{4,3,2,1,0:T(8,128)(2,1)} collective-permute-done((bf16[1,120,2,64,128]{4,3,2,1,0:T(8,128)(2,1)}, bf16[1,120,2,64,128]{4,3,2,1,0:T(8,128)(2,1)}, u32[]{:S(2)}, u32[]{:S(2)}) %collective-permute-start.2) | collective-permute-done | bytes 3932192 | tf_op jit(solution)/shard_map/ppermute | solution.py:10
  307.4 0.0 copy-done
  307.4 12.7 %fusion.6 = bf16[4,121,2,64,128]{4,3,2,1,0:T(8,128)(2,1)} fusion(bf16[1,120,2,64,128]{4,3,2,1,0:T(8,128)(2,1)} %collective-permute-done.2, bf16[1,120,2,64,128]{4,3,2,1,0:T(8,128)(2,1)} %collective-permute-done.1, bf16[1,120,2,64,128]{4,3,2,1,0:T(8,128)(2,1)} %collective-permute-done, bf16[1,120,2,64,128]{4,3,2,1,0:T(8,128)(2,1)S(1)} %copy-done), kind=kLoop, calls=%fused_computation.10 | loop fusion | flops 103088128 | bytes 31588352 | tf_op jit(solution)/shard_map/concatenate | solution.py:93
  320.1 8.8 %gather_fusion.2 = bf16[120,2,64,128]{3,2,1,0:T(8,128)(2,1)} fusion(bf16[4,121,2,64,128]{4,3,2,1,0:T(8,128)(2,1)} %fusion.6, s32[120]{0:T(128)S(1)} %reshape.401), kind=kCustom, calls=%fused_computation.2 | custom fusion | bytes 7865280 | tf_op jit(solution)/shard_map/gather | solution.py:115
  328.9 3.1 copy.87
  332.0 0.0 copy-start.2
  332.1 0.0 copy-done.4
  332.1 0.6 fusion.23
  332.7 1.3 copy-done.2
  334.0 0.7 fusion.24
  334.7 25.5 %gather_fusion = bf16[360,2,64,128]{3,2,1,0:T(8,128)(2,1)} fusion(bf16[4,121,2,64,128]{4,3,2,1,0:T(8,128)(2,1)} %fusion.6, s32[360]{0:T(512)S(1)} %reshape.389), kind=kCustom, calls=%fused_computation | custom fusion | bytes 23595840 | tf_op jit(solution)/shard_map/gather | solution.py:98
  360.1 6.5 %copy.75 = bf16[360,2,64,128]{3,2,0,1:T(8,128)(2,1)S(1)} copy(bf16[360,2,64,128]{3,2,1,0:T(8,128)(2,1)} %gather_fusion) | data formatting | bytes 23592960 | tf_op jit(solution)/shard_map/gather | solution.py:98
  366.7 0.0 copy-done.1
  366.7 1.7 fusion.27
  368.4 0.0 copy-start.3
  368.4 1.7 fusion.36
  370.0 0.4 copy-done.3
  370.5 0.7 fusion.54
  371.2 0.7 fusion.52
  371.8 1.7 fusion.42
  373.5 1.7 fusion.48
  375.2 0.7 maximum_add_fusion
  375.9 0.0 all-reduce.4.cloned.1.call-update
  375.9 22.9 %all-reduce.4.cloned.1.call-done = f32[1,3,2,64,64]{3,4,1,2,0:T(8,128)} async-done(((f32[1,3,2,64,64]{3,4,1,2,0:T(8,128)}), f32[1,3,2,64,64]{3,4,1,2,0:T(8,128)}) %all-reduce.4.cloned.1.call-update) | async-done | bytes 98320 | tf_op jit(solution)/shard_map/psum | solution.py:120
  398.8 1.0 constant_dynamic-slice_fusion
  399.9 0.8 copy.93
  (18 shorter events, 0.2 us)
Async XLA Ops:
  6.5 91.2 %collective-permute-start = (bf16[1,120,2,64,128]{4,3,2,1,0:T(8,128)(2,1)}, bf16[1,120,2,64,128]{4,3,2,1,0:T(8,128)(2,1)}, u32[]{:S(2)}, u32[]{:S(2)}) collective-permute-start(bf16[1,120,2,64,128]{4,3,2,1,0:T(8,128)(2,1)} %param.4), channel_id=1, source_target_pairs={{2,0},{4,2},{6,4},{8,6},{10,8},{12,10},{14,12},{16,14},{18,16},{20... | collective-permute-start | bytes 11796488 | tf_op jit(solution)/shard_map/ppermute | solution.py:10
  12.0 169.1 %collective-permute-start.1 = (bf16[1,120,2,64,128]{4,3,2,1,0:T(8,128)(2,1)}, bf16[1,120,2,64,128]{4,3,2,1,0:T(8,128)(2,1)}, u32[]{:S(2)}, u32[]{:S(2)}) collective-permute-start(bf16[1,120,2,64,128]{4,3,2,1,0:T(8,128)(2,1)} %param.4), channel_id=1, source_target_pairs={{8,0},{10,2},{12,4},{14,6},{16,8},{18,10},{20,12},{22,14},{24,16},... | collective-permute-start | bytes 11796488 | tf_op jit(solution)/shard_map/ppermute | solution.py:10
  12.5 294.9 %collective-permute-start.2 = (bf16[1,120,2,64,128]{4,3,2,1,0:T(8,128)(2,1)}, bf16[1,120,2,64,128]{4,3,2,1,0:T(8,128)(2,1)}, u32[]{:S(2)}, u32[]{:S(2)}) collective-permute-start(bf16[1,120,2,64,128]{4,3,2,1,0:T(8,128)(2,1)} %param.4), channel_id=1, source_target_pairs={{16,0},{18,2},{20,4},{22,6},{24,8},{26,10},{28,12},{30,14},{0,16},... | collective-permute-start | bytes 11796488 | tf_op jit(solution)/shard_map/ppermute | solution.py:10
  13.7 11.3 %all-to-all-start.1 = ((s32[3,2,1]{0,2,1:T(1,128)}), s32[3,2,1]{0,2,1:T(1,128)S(1)}, u32[]{:S(2)}, u32[]{:S(2)}) async-start(s32[3,2,1]{0,2,1:T(1,128)} %broadcast_in_dim.35), calls=%async_computation.1 | async-start | bytes 2048 | tf_op jit(solution)/shard_map/all_to_all | solution.py:114
  25.0 13.8 %all-to-all-start.2 = ((s32[3,2,20]{2,0,1:T(4,128)}), s32[3,2,20]{2,0,1:T(4,128)S(1)}, u32[]{:S(2)}, u32[]{:S(2)}) async-start(s32[3,2,20]{2,0,1:T(4,128)} %copy.85), calls=%async_computation.2 | async-start | bytes 8192 | tf_op jit(solution)/shard_map/all_to_all | solution.py:113
  38.9 49.9 %all-to-all-start = ((bf16[3,40,2,64,128]{4,3,0,2,1:T(8,128)(2,1)}), bf16[3,40,2,64,128]{4,3,0,2,1:T(8,128)(2,1)}, u32[]{:S(2)}, u32[]{:S(2)}) async-start(bf16[3,40,2,64,128]{4,3,0,2,1:T(8,128)(2,1)} %copy.81), calls=%async_computation | async-start | bytes 7864320 | tf_op jit(solution)/shard_map/all_to_all | solution.py:112
  44.4 354.5 %all-reduce.4.cloned.1.call-start = ((), (), s32[]{:S(2)}) async-start(), calls=%async_computation.3 | async-start | bytes 393216 | tf_op jit(solution)/shard_map/psum | solution.py:120
  88.7 218.6 %copy-start = (bf16[1,120,2,64,128]{4,3,2,1,0:T(8,128)(2,1)S(1)}, bf16[1,120,2,64,128]{4,3,2,1,0:T(8,128)(2,1)}, u32[]{:S(2)}) copy-start(bf16[1,120,2,64,128]{4,3,2,1,0:T(8,128)(2,1)} %param.4) | copy-start | bytes 11796484
  328.9 3.2 copy-start.4
  332.0 2.0 copy-start.2
  360.1 6.5 %copy-start.1 = (bf16[1,120,2,64,128]{4,3,2,1,0:T(8,128)(2,1)S(1)}, bf16[1,120,2,64,128]{4,3,2,1,0:T(8,128)(2,1)}, u32[]{:S(2)}) copy-start(bf16[1,120,2,64,128]{4,3,2,1,0:T(8,128)(2,1)} %param.4) | copy-start | bytes 11796484
  368.4 2.1 copy-start.3
Sparse Core Ops, SparseCore 0:
  376.0 22.7 all-reduce.3
where the time goes:
time: 408 us; the launch traced here: 407 us
  waiting for transfers between devices  281 us (69%)
  local copies, waits for them, and re-layouts  64.7 us (16%)
  other arithmetic  21 us (5%)
  starting transfers between devices  18.1 us (4%)
  between operations  13.6 us (3%)
  matrix products  9.31 us (2%)
    ppermute x3, waiting for transfers between devices, shifted(): return lax.ppermute(block, axis, route)  214 us
    all_to_all x1, waiting for transfers between devices, on_device(): lax.all_to_all(payload, 'ga', split_axis=1, concat_axis=1, tiled=True)  43.7 us
    gather x2, local copies, waits for them, and re-layouts, on_device(): ket_self = kets[ket_index[:, None], self_place]  32 us
    psum x1, waiting for transfers between devices, on_device(): total = lax.psum(summed_part, 'ga')  22.9 us
    concatenate x1, other arithmetic, on_device(): jnp.concatenate([coeffs, row_point, plane_kets, opposite], axis=0)  12.7 us
    gather x2, local copies, waits for them, and re-layouts, on_device(): partner = kets[owners[:, 0][:, None], places_in]  12 us
    gather x2, local copies, waits for them, and re-layouts, on_device(): payload = coeffs[bra_index[:, None], sent_block]  10.5 us
  transfers between devices with their start and end apart: 7, of which 5 were waited for; matrix products, arithmetic and copies ran while one was open for 6% of the time, Pallas kernels for 0%

commit v1 on v0

--- a/solution.py
+++ b/solution.py
@@ -1,7 +1,13 @@
+import functools
+
 import jax
 import jax.numpy as jnp
 from jax import lax
 from jax.sharding import PartitionSpec as P
+from jax.experimental import pallas as pl
+from jax.experimental.pallas import tpu as pltpu
+
+CHUNKS = 4
 
 
 def shifted(block, axis, distance):
@@ -122,9 +128,208 @@
     return lax.dynamic_slice_in_dim(total, my_slice * row_count, row_count, 3)
 
 
+def gather_kernel(count, index_ref, source_ref, out_ref, sems):
+    def copy(i):
+        return pltpu.make_async_copy(source_ref.at[index_ref[i]], out_ref.at[i], sems.at[i])
+
+    def begin(i, carry):
+        copy(i).start()
+        return carry
+
+    def finish(i, carry):
+        copy(i).wait()
+        return carry
+
+    lax.fori_loop(0, count, begin, 0)
+    lax.fori_loop(0, count, finish, 0)
+
+
+def gather_blocks(index, source):
+    count = index.shape[0]
+    shape = (count,) + source.shape[1:]
+    return pl.pallas_call(
+        functools.partial(gather_kernel, count),
+        out_shape=jax.ShapeDtypeStruct(shape, source.dtype),
+        in_specs=[
+            pl.BlockSpec(memory_space=pltpu.SMEM),
+            pl.BlockSpec(memory_space=pl.ANY),
+        ],
+        out_specs=pl.BlockSpec(memory_space=pltpu.VMEM),
+        scratch_shapes=[pltpu.SemaphoreType.DMA((count,))],
+        name="gather_blocks",
+        cost_estimate=pl.CostEstimate(flops=0, bytes_accessed=4 * source.dtype.itemsize * count * source[0].size, transcendentals=0),
+    )(index, source)
+
+
+def dot_kernel(edges, items, starts, *refs):
+    count = len(starts)
+    left_ref, right_ref = refs[0], refs[1]
+    parts = refs[2 : 2 + count]
+    out_ref, held, sems = refs[2 + count :]
+    rows = held.shape[1] * held.shape[2]
+    bands = held.shape[2]
+    lanes = held.shape[3]
+    copies = []
+    for n, part in enumerate(parts):
+        copy = pltpu.make_async_copy(part, held.at[pl.ds(starts[n], part.shape[0])], sems.at[n])
+        copy.start()
+        copies.append(copy)
+    for copy in copies:
+        copy.wait()
+    unroll = 8 if items % 8 == 0 else 2
+
+    for e in range(edges):
+        def step(i, total):
+            for u in range(0, unroll, 2):
+                at = e * items + i * unroll + u
+                left = jnp.concatenate(
+                    [held[left_ref[at]].reshape(rows, lanes), held[left_ref[at + 1]].reshape(rows, lanes)], axis=1
+                )
+                right = jnp.concatenate(
+                    [held[right_ref[at]].reshape(rows, lanes), held[right_ref[at + 1]].reshape(rows, lanes)], axis=1
+                )
+                total = total + lax.dot_general(
+                    left, right, (((1,), (1,)), ((), ())), preferred_element_type=jnp.float32
+                )
+            return total
+
+        total = lax.fori_loop(0, items // unroll, step, jnp.zeros((rows, rows), jnp.float32))
+        out_ref[e, 0] = total[:bands, :bands] + total[bands:, bands:]
+        out_ref[e, 1] = total[:bands, bands:] - total[bands:, :bands]
+
+
+def dot_items(left, right, parts):
+    edges, items = left.shape
+    bands, lanes = parts[0].shape[2], parts[0].shape[3]
+    starts, blocks = [], 0
+    for part in parts:
+        starts.append(blocks)
+        blocks += part.shape[0]
+    nbytes = blocks * parts[0][0].size * parts[0].dtype.itemsize
+    return pl.pallas_call(
+        functools.partial(dot_kernel, edges, items, tuple(starts)),
+        out_shape=jax.ShapeDtypeStruct((edges, 2, bands, bands), jnp.float32),
+        in_specs=[pl.BlockSpec(memory_space=pltpu.SMEM)] * 2
+        + [pl.BlockSpec(memory_space=pl.ANY)] * len(parts),
+        out_specs=pl.BlockSpec(memory_space=pltpu.VMEM),
+        scratch_shapes=[
+            pltpu.VMEM((blocks,) + parts[0].shape[1:], parts[0].dtype),
+            pltpu.SemaphoreType.DMA((len(parts),)),
+        ],
+        compiler_params=pltpu.CompilerParams(vmem_limit_bytes=nbytes + 8 * 2**20),
+        name="dot_items",
+        cost_estimate=pl.CostEstimate(
+            flops=edges * items * 2 * 4 * bands * bands * lanes, bytes_accessed=nbytes, transcendentals=0
+        ),
+    )(left.reshape(-1), right.reshape(-1), *parts)
+
+
+def on_four_rows(coeffs, neighbour, shift_id, block_map):
+    own = coeffs[0]
+    slab = own.shape[0]
+    points = lax.axis_size("ka")
+    row = points // 4
+    me = lax.axis_index("ka")
+    mine = lax.axis_index("ga")
+    column = jnp.mod(me, row)
+    even = jnp.mod(column, 2) == 0
+    capacity = 2 * max(1, slab // 12)
+
+    down, up = [], []
+    for k in range(points):
+        z, i = k // row, k % row
+        if i % 2 == 0 or z in (1, 2):
+            down.append(((k + row) % points, k))
+        if i % 2 == 1 or z in (0, 3):
+            up.append(((k - row) % points, k))
+    direct = [(k + 1, k) for k in range(points) if k % row < row - 1]
+    around = [(k - (row - 1), k) for k in range(points) if k % row == row - 1]
+    to_lower = [((k + row) % points, k) for k in range(points)]
+    to_upper = [((k - row) % points, k) for k in range(points)]
+    swap = [(0, 1), (1, 0)]
+
+    def role_shift(step):
+        return jnp.sum(jnp.where(neighbour[0] == jnp.mod(me + step, points), shift_id[0], 0))
+
+    row_shift, half_shift = role_shift(row), role_shift(points // 2)
+    sent = jnp.stack([row_shift, half_shift])
+    lower = lax.ppermute(sent, "ka", to_upper)
+    upper = lax.ppermute(sent, "ka", to_lower)
+    shifts = jnp.stack([role_shift(1), jnp.where(even, row_shift, lower[0]), lower[1], upper[1]])
+
+    picks = shifts[:, None] == jnp.arange(block_map.shape[0], dtype=jnp.int32)[None, :]
+    relabel = jnp.sum(jnp.where(picks[:, :, None], block_map[None], 0), axis=1)
+    by_slice = relabel.reshape(relabel.shape[0], 2, slab)
+    first = mine == 0
+    here = jnp.where(first, by_slice[:, 0], by_slice[:, 1])
+    there = jnp.where(first, by_slice[:, 1], by_slice[:, 0])
+    crosses_here = (here // slab) != mine
+    crosses_there = (there // slab) == mine
+    rank_here = jnp.cumsum(crosses_here.astype(jnp.int32), axis=1) - 1
+    rank_there = jnp.cumsum(crosses_there.astype(jnp.int32), axis=1) - 1
+    places = jnp.arange(capacity, dtype=jnp.int32)
+    match_here = crosses_here[:, None, :] & (rank_here[:, None, :] == places[None, :, None])
+    match_there = crosses_there[:, None, :] & (rank_there[:, None, :] == places[None, :, None])
+    lanes = jnp.arange(slab, dtype=jnp.int32)
+    bra_sent = jnp.sum(jnp.where(match_here, lanes[None, None, :], 0), axis=2)
+    ket_sent = jnp.sum(jnp.where(match_there, (there - mine * slab)[:, None, :], 0), axis=2)
+    ket_at = jnp.sum(jnp.where(match_here, ket_sent[:, :, None], 0), axis=1)
+    sends_bra = jnp.stack([even | True, even, even | True, even & False])
+    send = jnp.where(sends_bra[:, None], bra_sent, ket_sent)
+
+    up_base, low_base, next_base, around_base, got_base = (slab * n for n in (1, 2, 3, 4, 5))
+    bra_base = jnp.stack([0, jnp.where(even, 0, low_base), low_base, up_base])
+    ket_base = jnp.stack(
+        [jnp.where(column == row - 1, around_base, next_base), jnp.where(even, up_base, 0), up_base, low_base]
+    )
+    got = got_base + capacity * jnp.arange(4, dtype=jnp.int32)[:, None] + rank_here
+    bra_home = bra_base[:, None] + lanes[None, :]
+    ket_home = ket_base[:, None] + here - mine * slab
+    left = jnp.where(crosses_here & sends_bra[:, None], got, bra_home)
+    right = jnp.where(
+        crosses_here, jnp.where(sends_bra[:, None], ket_base[:, None] + ket_at, got), ket_home
+    )
+
+    size = slab // CHUNKS
+    upper_parts = [lax.ppermute(own[c * size : (c + 1) * size], "ka", down) for c in range(CHUNKS)]
+    lower_part = lax.ppermute(own, "ka", up)
+    next_part = lax.ppermute(own, "ka", direct)
+    around_parts = [lax.ppermute(part, "ka", around) for part in upper_parts]
+    got_own = lax.ppermute(gather_blocks(send[:2].reshape(-1), own), "ga", swap)
+    got_lower = lax.ppermute(gather_blocks(send[2:].reshape(-1), lower_part), "ga", swap)
+    sums = dot_items(
+        left, right, [own, *upper_parts, lower_part, next_part, *around_parts, got_own, got_lower]
+    )
+
+    half = sums.shape[2] // 2
+    low_rows, high_rows = sums[:, :, :half], sums[:, :, half:]
+    kept = jnp.where(first, low_rows, high_rows)
+    total = kept + lax.ppermute(jnp.where(first, high_rows, low_rows), "ga", swap)
+    from_upper = lax.ppermute(total[1:3], "ka", to_lower)
+    from_lower = lax.ppermute(total[3], "ka", to_upper)
+    row_sum = jnp.where(even, total[1], from_upper[0])
+    half_sum = from_upper[1] + from_lower
+    target = neighbour[0][:, None, None, None]
+    out = jnp.where(
+        target == jnp.mod(me + 1, points),
+        total[0],
+        jnp.where(target == jnp.mod(me + row, points), row_sum, half_sum),
+    )
+    return out[None]
+
+
 def solution(mesh):
     in_specs = (P("ka", "ga", None, None, None), P("ka", None), P("ka", None), P())
     out_specs = P("ka", None, None, "ga", None)
-    return jax.shard_map(
-        on_device, mesh=mesh, in_specs=in_specs, out_specs=out_specs, check_vma=False
-    )
+    four_rows = mesh.shape["ga"] == 2 and mesh.shape["ka"] == 4 * min(16, mesh.shape["ka"] // 4)
+
+    def run(coeffs, neighbour, shift_id, block_map):
+        one_each = coeffs.shape[0] == mesh.shape["ka"]
+        per_slice = coeffs.shape[1] // mesh.shape["ga"]
+        whole_chunks = per_slice % (2 * CHUNKS) == 0 or per_slice % CHUNKS == 0 and per_slice % 2 == 0
+        body = on_four_rows if four_rows and one_each and whole_chunks else on_device
+        return jax.shard_map(
+            body, mesh=mesh, in_specs=in_specs, out_specs=out_specs, check_vma=False
+        )(coeffs, neighbour, shift_id, block_map)
+
+    return run

time: 408 us -> 252 us (0.62)
  waiting for transfers between devices: 281 us -> 114 us
  starting transfers between devices: 18.1 us -> 89.6 us
  local copies, waits for them, and re-layouts: 64.7 us -> 11.3 us
  Pallas kernels: 0 us -> 27.4 us
  other arithmetic: 21 us -> 7.32 us
  between operations: 13.6 us -> 1.46 us
  matrix products: 9.31 us -> 0 us
    ppermute x3 -> x17, waiting for transfers between devices: 214 us -> 114 us  [the longest x1 71.7 us: on_four_rows(): lower = lax.ppermute(sent, 'ka', to_upper)]
    ppermute x3 -> x17, starting transfers between devices: 5.92 us -> 89.6 us  [the longest x4 37.4 us: on_four_rows(): lax.ppermute(own[c * size:(c + 1) * size], 'ka', down)]
    gather x6 -> x0, local copies, waits for them, and re-layouts: 54.4 us -> none  [the longest x2 32 us: on_device(): ket_self = kets[ket_index[:, None], self_place]]
    all_to_all x3 -> x0, waiting for transfers between devices: 43.7 us -> none  [the longest x1 43.7 us: on_device(): lax.all_to_all(payload, 'ga', split_axis=1, concat_axis=1, tiled=True)]
    pallas_call x0 -> x3, Pallas kernels: none -> 27.4 us  [the longest x1 20.7 us: dot_items(): pl.pallas_call(functools.partial(dot_kernel, edges, items, tuple(starts))...]
    psum x1 -> x0, waiting for transfers between devices: 22.9 us -> none  [on_device(): total = lax.psum(summed_part, 'ga')]
    concatenate x6 -> x0, other arithmetic: 13.6 us -> none  [the longest x1 12.7 us: on_device(): jnp.concatenate([coeffs, row_point, plane_kets, opposite], axis=0)]
    all_to_all x3 -> x0, starting transfers between devices: 11.9 us -> none  [the longest x1 5.5 us: on_device(): lax.all_to_all(payload, 'ga', split_axis=1, concat_axis=1, tiled=True)]
  transfers between devices with their start and end apart: 7 -> 17, of which waited for: 5 -> 8; matrix products, arithmetic and copies ran while one was open for 6% -> 6% of each run, Pallas kernels for 0% -> 3%
where the time goes in v1:
time: 252 us; the launch traced here: 251 us
  waiting for transfers between devices  114 us (45%)
  starting transfers between devices  89.6 us (36%)
  Pallas kernels  27.4 us (11%)
  local copies, waits for them, and re-layouts  11.3 us (4%)
  other arithmetic  7.32 us (3%)
    ppermute x1, waiting for transfers between devices, on_four_rows(): lower = lax.ppermute(sent, 'ka', to_upper)  71.7 us
    ppermute x4, starting transfers between devices, on_four_rows(): lax.ppermute(own[c * size:(c + 1) * size], 'ka', down)  37.4 us
    ppermute x1, starting transfers between devices, on_four_rows(): from_upper = lax.ppermute(total[1:3], 'ka', to_lower)  27.9 us
    ppermute x4, waiting for transfers between devices, on_four_rows(): around_parts = [lax.ppermute(part, 'ka', around) for part in upper_parts]  26.6 us
    pallas_call x1, Pallas kernels, dot_items(): pl.pallas_call(functools.partial(dot_kernel, edges, items, tuple(starts))...  20.7 us
    ppermute x4, starting transfers between devices, on_four_rows(): around_parts = [lax.ppermute(part, 'ka', around) for part in upper_parts]  9.1 us
    pallas_call x2, Pallas kernels, gather_blocks(): pl.pallas_call(functools.partial(gather_kernel, count), out_shape=jax.Sha...  6.74 us
  transfers between devices with their start and end apart: 17, of which 8 were waited for; matrix products, arithmetic and copies ran while one was open for 6% of the time, Pallas kernels for 3%

profile of v1, /device:TPU:0, one launch (start us, length us, event | category | flops | bytes accessed | tf_op | source)
XLA Modules:
  0.0 251.1 jit_solution(15798769652162001281)
XLA Ops:
  0.0 1.3 collective-permute-start.6
  1.3 1.3 fusion.15
  2.7 1.3 pad_add_fusion.1
  4.0 4.2 %collective-permute-start = (s32[2]{0:T(128)S(1)}, s32[2]{0:T(128)S(1)}, u32[]{:S(2)}, u32[]{:S(2)}) collective-permute-start(s32[2]{0:T(128)S(1)} %pad_add_fusion.1), channel_id=1, source_target_pairs={{24,0},{26,2},{28,4},{30,6},{0,8},{2,10},{4,12},{6,14},{8,16},{10,... | collective-permute-start | bytes 32 | tf_op jit(solution)/shard_map/ppermute | solution.py:256
  8.2 1.5 collective-permute-start.1
  9.7 1.3 collective-permute-start.7
  11.0 4.5 %slice_bitcast_fusion = (bf16[30,2,64,128]{3,2,1,0:T(8,128)(2,1)}, bf16[30,2,64,128]{3,2,1,0:T(8,128)(2,1)}, bf16[30,2,64,128]{3,2,1,0:T(8,128)(2,1)S(1)}, bf16[30,2,64,128]{3,2,1,0:T(8,128)(2,1)}) fusion(bf16[1,120,2,64,128]{4,3,2,1,0:T(8,128)(2,1)} %param.4), kind=kLoop, calls=%fused_computation | loop fusion | bytes 7864320 | tf_op jit(solution)/shard_map/slice | solution.py:294
  15.5 5.7 %collective-permute-start.4 = (bf16[30,2,64,128]{3,2,1,0:T(8,128)(2,1)}, bf16[30,2,64,128]{3,2,1,0:T(8,128)(2,1)}, u32[]{:S(2)}, u32[]{:S(2)}) collective-permute-start(bf16[30,2,64,128]{3,2,1,0:T(8,128)(2,1)} %get-tuple-element.20), channel_id=1, source_target_pairs={{8,0},{12,4},{16,8},{18,10},{20,12},{22,14},{24,16},{26,18},{28,20... | collective-permute-start | bytes 2949128 | tf_op jit(solution)/shard_map/ppermute | solution.py:294
  21.3 0.1 pad_add_fusion
  21.4 71.7 %collective-permute-done = s32[2]{0:T(128)S(1)} collective-permute-done((s32[2]{0:T(128)S(1)}, s32[2]{0:T(128)S(1)}, u32[]{:S(2)}, u32[]{:S(2)}) %collective-permute-start) | collective-permute-done | bytes 40 | tf_op jit(solution)/shard_map/ppermute | solution.py:256
  93.1 13.3 %collective-permute-start.5 = (bf16[30,2,64,128]{3,2,1,0:T(8,128)(2,1)}, bf16[30,2,64,128]{3,2,1,0:T(8,128)(2,1)S(1)}, u32[]{:S(2)}, u32[]{:S(2)}) collective-permute-start(bf16[30,2,64,128]{3,2,1,0:T(8,128)(2,1)} %get-tuple-element.17), channel_id=1, source_target_pairs={{8,0},{12,4},{16,8},{18,10},{20,12},{22,14},{24,16},{26,18},{28,20... | collective-permute-start | bytes 2949128 | tf_op jit(solution)/shard_map/ppermute | solution.py:294
  106.4 0.6 fusion.22
  108.3 0.6 slice.73
  108.8 1.9 pad_add_fusion.2
  110.7 0.1 iota_compare_fusion.2
  110.8 0.1 select_reduce_fusion.3
  110.9 0.1 reshape.119
  111.0 0.3 reduce_window_sum.21
  111.3 0.3 reduce_window_sum.19
  111.7 0.1 broadcast_add_fusion.1
  111.7 0.4 select_reduce_fusion.2
  112.1 0.5 select_reduce_fusion
  112.6 0.1 fusion.20
  112.7 0.1 copy.9
  112.8 0.6 reshape.120.index_ref
  113.4 3.4 %gather_blocks.2 = bf16[40,2,64,128]{3,2,1,0:T(8,128)(2,1)} custom-call(s32[40]{0:T(128)} %reshape.120.index_ref, bf16[120,2,64,128]{3,2,1,0:T(8,128)(2,1)} %bitcast.65), custom_call_target="tpu_custom_call" | custom-call | bytes 5242880 | tf_op jit(solution)/shard_map/gather_blocks/pallas_call | solution.py:150
  116.8 1.6 collective-permute-start.12
  118.3 1.9 collective-permute-start.2
  120.3 16.5 %collective-permute-start.3 = (bf16[30,2,64,128]{3,2,1,0:T(8,128)(2,1)}, bf16[30,2,64,128]{3,2,1,0:T(8,128)(2,1)}, u32[]{:S(2)}, u32[]{:S(2)}) collective-permute-start(bf16[30,2,64,128]{3,2,1,0:T(8,128)(2,1)} %get-tuple-element.18), channel_id=1, source_target_pairs={{8,0},{12,4},{16,8},{18,10},{20,12},{22,14},{24,16},{26,18},{28,20... | collective-permute-start | bytes 2949128 | tf_op jit(solution)/shard_map/ppermute | solution.py:294
  136.7 0.0 collective-permute-done.6.source_ref.refs_7_
  136.8 2.3 collective-permute-start.10
  139.0 0.1 copy.10
  139.1 0.7 reshape.121.index_ref
  139.8 3.4 %gather_blocks.3 = bf16[40,2,64,128]{3,2,1,0:T(8,128)(2,1)} custom-call(s32[40]{0:T(128)} %reshape.121.index_ref, bf16[120,2,64,128]{3,2,1,0:T(8,128)(2,1)} %collective-permute-done.6.source_ref.refs_7_), custom_call_target="tpu_custom_call" | custom-call | bytes 5242880 | tf_op jit(solution)/shard_map/gather_blocks/pallas_call | solution.py:150
  143.2 0.0 collective-permute-done.2.refs_3_
  143.2 1.8 collective-permute-start.13
  145.0 4.1 %collective-permute-done.3.refs_4_ = bf16[30,2,64,128]{3,2,1,0:T(8,128)(2,1)} collective-permute-done((bf16[30,2,64,128]{3,2,1,0:T(8,128)(2,1)}, bf16[30,2,64,128]{3,2,1,0:T(8,128)(2,1)}, u32[]{:S(2)}, u32[]{:S(2)}) %collective-permute-start.3) | collective-permute-done | bytes 983072 | tf_op jit(solution)/shard_map/ppermute | solution.py:294
  149.1 2.3 collective-permute-start.11
  151.4 2.3 collective-permute-start.8
  153.6 2.3 collective-permute-start.9
  155.9 0.1 pad_add_fusion.3
  156.0 0.1 iota_add_fusion
  156.1 0.1 add.126
  156.2 0.1 add.127
  156.2 0.1 add.128
  156.3 0.1 and.79
  156.4 0.1 and.80
  156.5 0.1 select_n.180
  156.6 0.1 reduce_sum.71
  156.6 0.1 add.122
  156.8 5.5 %collective-permute-done.11.refs_12_ = bf16[30,2,64,128]{3,2,1,0:T(8,128)(2,1)} collective-permute-done((bf16[30,2,64,128]{3,2,1,0:T(8,128)(2,1)}, bf16[30,2,64,128]{3,2,1,0:T(8,128)(2,1)}, u32[]{:S(2)}, u32[]{:S(2)}) %collective-permute-start.11) | collective-permute-done | bytes 983072 | tf_op jit(solution)/shard_map/ppermute | solution.py:297
  162.3 10.5 %collective-permute-done.8.refs_9_ = bf16[30,2,64,128]{3,2,1,0:T(8,128)(2,1)} collective-permute-done((bf16[30,2,64,128]{3,2,1,0:T(8,128)(2,1)}, bf16[30,2,64,128]{3,2,1,0:T(8,128)(2,1)}, u32[]{:S(2)}, u32[]{:S(2)}) %collective-permute-start.8) | collective-permute-done | bytes 983072 | tf_op jit(solution)/shard_map/ppermute | solution.py:297
  172.8 10.5 %collective-permute-done.9.refs_10_ = bf16[30,2,64,128]{3,2,1,0:T(8,128)(2,1)} collective-permute-done((bf16[30,2,64,128]{3,2,1,0:T(8,128)(2,1)}, bf16[30,2,64,128]{3,2,1,0:T(8,128)(2,1)}, u32[]{:S(2)}, u32[]{:S(2)}) %collective-permute-start.9) | collective-permute-done | bytes 983072 | tf_op jit(solution)/shard_map/ppermute | solution.py:297
  183.4 0.0 collective-permute-done.7.refs_8_
  183.4 2.1 copy-done
  185.5 1.2 copy-done.2
  186.7 20.7 %dot_items.1 = f32[4,2,64,64]{3,2,1,0:T(8,128)S(1)} custom-call(s32[480]{0:T(512)S(1)} %get-tuple-element.27.refs_0_, s32[480]{0:T(512)S(1)} %get-tuple-element.26.refs_1_, bf16[120,2,64,128]{3,2,1,0:T(8,128)(2,1)S(1)} %bitcast.66, bf16[30,2,64,128]{3,2,1,0:T(8,128)(2,1)} %collective-permute-done.2.refs_3_, ...), custom_call_target="tpu_custom_call" | custom-call | flops 2013265920 | bytes 22282240 | tf_op jit(solution)/shard_map/dot_items/pallas_call | solution.py:209
  207.4 1.5 collective-permute-start.14
  209.0 3.5 %collective-permute-done.14 = f32[4,2,32,64]{3,2,1,0:T(8,128)S(1)} collective-permute-done((f32[4,2,32,64]{3,2,1,0:T(8,128)S(1)}, f32[4,2,32,64]{3,2,1,0:T(8,128)S(1)}, u32[]{:S(2)}, u32[]{:S(2)}) %collective-permute-start.14) | collective-permute-done | bytes 65568 | tf_op jit(solution)/shard_map/ppermute | solution.py:307
  212.5 27.9 %collective-permute-start.15 = (f32[2,2,32,64]{3,2,1,0:T(8,128)S(1)}, f32[2,2,32,64]{3,2,1,0:T(8,128)S(1)}, u32[]{:S(2)}, u32[]{:S(2)}) collective-permute-start(f32[2,2,32,64]{3,2,1,0:T(8,128)S(1)} %slice.102), channel_id=1, source_target_pairs={{8,0},{10,2},{12,4},{14,6},{16,8},{18,10},{20,12},{22,14},{24,16},... | collective-permute-start | bytes 98312 | tf_op jit(solution)/shard_map/ppermute | solution.py:308
  240.4 4.2 %collective-permute-done.15 = f32[2,2,32,64]{3,2,1,0:T(8,128)S(1)} collective-permute-done((f32[2,2,32,64]{3,2,1,0:T(8,128)S(1)}, f32[2,2,32,64]{3,2,1,0:T(8,128)S(1)}, u32[]{:S(2)}, u32[]{:S(2)}) %collective-permute-start.15) | collective-permute-done | bytes 32800 | tf_op jit(solution)/shard_map/ppermute | solution.py:308
  244.6 2.1 collective-permute-start.16
  246.6 3.7 %collective-permute-done.16 = f32[2,32,64]{2,1,0:T(8,128)S(1)} collective-permute-done((f32[2,32,64]{2,1,0:T(8,128)S(1)}, f32[2,32,64]{2,1,0:T(8,128)S(1)}, u32[]{:S(2)}, u32[]{:S(2)}) %collective-permute-start.16) | collective-permute-done | bytes 16416 | tf_op jit(solution)/shard_map/ppermute | solution.py:309
  250.3 0.7 select_select_fusion
  (25 shorter events, 0.2 us)
Async XLA Ops:
  0.0 136.7 %collective-permute-start.6 = (bf16[120,2,64,128]{3,2,1,0:T(8,128)(2,1)}, bf16[120,2,64,128]{3,2,1,0:T(8,128)(2,1)}, u32[]{:S(2)}, u32[]{:S(2)}) collective-permute-start(bf16[120,2,64,128]{3,2,1,0:T(8,128)(2,1)} %bitcast.63), channel_id=1, source_target_pairs={{24,0},{26,2},{28,4},{30,6},{2,10},{6,14},{10,18},{14,22},{16,24},... | collective-permute-start | bytes 11796488 | tf_op jit(solution)/shard_map/ppermute | solution.py:295
  4.0 106.8 %copy-start.3 = (s32[8,240]{1,0:T(8,128)S(1)}, s32[8,240]{1,0:T(8,128)}, u32[]{:S(2)}) copy-start(s32[8,240]{1,0:T(8,128)} %param.7) | copy-start | bytes 23044
  4.0 89.2 %collective-permute-start = (s32[2]{0:T(128)S(1)}, s32[2]{0:T(128)S(1)}, u32[]{:S(2)}, u32[]{:S(2)}) collective-permute-start(s32[2]{0:T(128)S(1)} %pad_add_fusion.1), channel_id=1, source_target_pairs={{24,0},{26,2},{28,4},{30,6},{0,8},{2,10},{4,12},{6,14},{8,16},{10,... | collective-permute-start | bytes 32 | tf_op jit(solution)/shard_map/ppermute | solution.py:256
  8.2 100.0 %collective-permute-start.1 = (s32[2]{0:T(128)S(1)}, s32[2]{0:T(128)S(1)}, u32[]{:S(2)}, u32[]{:S(2)}) collective-permute-start(s32[2]{0:T(128)S(1)} %pad_add_fusion.1), channel_id=1, source_target_pairs={{8,0},{10,2},{12,4},{14,6},{16,8},{18,10},{20,12},{22,14},{24,16},... | collective-permute-start | bytes 32 | tf_op jit(solution)/shard_map/ppermute | solution.py:257
  9.7 173.6 %collective-permute-start.7 = (bf16[120,2,64,128]{3,2,1,0:T(8,128)(2,1)}, bf16[120,2,64,128]{3,2,1,0:T(8,128)(2,1)}, u32[]{:S(2)}, u32[]{:S(2)}) collective-permute-start(bf16[120,2,64,128]{3,2,1,0:T(8,128)(2,1)} %bitcast.64), channel_id=1, source_target_pairs={{2,0},{4,2},{6,4},{10,8},{12,10},{14,12},{18,16},{20,18},{22,20},{... | collective-permute-start | bytes 11796488 | tf_op jit(solution)/shard_map/ppermute | solution.py:296
  15.5 102.8 %collective-permute-start.4 = (bf16[30,2,64,128]{3,2,1,0:T(8,128)(2,1)}, bf16[30,2,64,128]{3,2,1,0:T(8,128)(2,1)}, u32[]{:S(2)}, u32[]{:S(2)}) collective-permute-start(bf16[30,2,64,128]{3,2,1,0:T(8,128)(2,1)} %get-tuple-element.20), channel_id=1, source_target_pairs={{8,0},{12,4},{16,8},{18,10},{20,12},{22,14},{24,16},{26,18},{28,20... | collective-permute-start | bytes 2949128 | tf_op jit(solution)/shard_map/ppermute | solution.py:294
  93.1 27.1 %collective-permute-start.5 = (bf16[30,2,64,128]{3,2,1,0:T(8,128)(2,1)}, bf16[30,2,64,128]{3,2,1,0:T(8,128)(2,1)S(1)}, u32[]{:S(2)}, u32[]{:S(2)}) collective-permute-start(bf16[30,2,64,128]{3,2,1,0:T(8,128)(2,1)} %get-tuple-element.17), channel_id=1, source_target_pairs={{8,0},{12,4},{16,8},{18,10},{20,12},{22,14},{24,16},{26,18},{28,20... | collective-permute-start | bytes 2949128 | tf_op jit(solution)/shard_map/ppermute | solution.py:294
  116.8 34.6 %collective-permute-start.12 = (bf16[40,2,64,128]{3,2,1,0:T(8,128)(2,1)}, bf16[40,2,64,128]{3,2,1,0:T(8,128)(2,1)S(1)}, u32[]{:S(2)}, u32[]{:S(2)}) collective-permute-start(bf16[40,2,64,128]{3,2,1,0:T(8,128)(2,1)} %gather_blocks.2), channel_id=1, source_target_pairs={{0,1},{1,0},{2,3},{3,2},{4,5},{5,4},{6,7},{7,6},{8,9},{9,8},{10,11... | collective-permute-start | bytes 3932168 | tf_op jit(solution)/shard_map/ppermute | solution.py:298
  118.3 24.9 %collective-permute-start.2 = (bf16[30,2,64,128]{3,2,1,0:T(8,128)(2,1)S(1)}, bf16[30,2,64,128]{3,2,1,0:T(8,128)(2,1)}, u32[]{:S(2)}, u32[]{:S(2)}) collective-permute-start(bf16[30,2,64,128]{3,2,1,0:T(8,128)(2,1)S(1)} %get-tuple-element.19), channel_id=1, source_target_pairs={{8,0},{12,4},{16,8},{18,10},{20,12},{22,14},{24,16},{26,18},{28,20... | collective-permute-start | bytes 2949128 | tf_op jit(solution)/shard_map/ppermute | solution.py:294
  120.3 22.9 %copy-start.1 = (bf16[30,2,64,128]{3,2,1,0:T(8,128)(2,1)}, bf16[30,2,64,128]{3,2,1,0:T(8,128)(2,1)S(1)}, u32[]{:S(2)}) copy-start(bf16[30,2,64,128]{3,2,1,0:T(8,128)(2,1)S(1)} %collective-permute-done.5.refs_6_) | copy-start | bytes 2949124
  120.3 28.8 %collective-permute-start.3 = (bf16[30,2,64,128]{3,2,1,0:T(8,128)(2,1)}, bf16[30,2,64,128]{3,2,1,0:T(8,128)(2,1)}, u32[]{:S(2)}, u32[]{:S(2)}) collective-permute-start(bf16[30,2,64,128]{3,2,1,0:T(8,128)(2,1)} %get-tuple-element.18), channel_id=1, source_target_pairs={{8,0},{12,4},{16,8},{18,10},{20,12},{22,14},{24,16},{26,18},{28,20... | collective-permute-start | bytes 2949128 | tf_op jit(solution)/shard_map/ppermute | solution.py:294
  136.8 16.9 %collective-permute-start.10 = (bf16[30,2,64,128]{3,2,1,0:T(8,128)(2,1)}, bf16[30,2,64,128]{3,2,1,0:T(8,128)(2,1)}, u32[]{:S(2)}, u32[]{:S(2)}) collective-permute-start(bf16[30,2,64,128]{3,2,1,0:T(8,128)(2,1)} %collective-permute-done.4.refs_5_), channel_id=1, source_target_pairs={{0,6},{8,14},{16,22},{24,30},{1,7},{9,15},{17,23},{25,31}} | collective-permute-start | bytes 2949128 | tf_op jit(solution)/shard_map/ppermute | solution.py:297
  143.2 40.2 %collective-permute-start.13 = (bf16[40,2,64,128]{3,2,1,0:T(8,128)(2,1)}, bf16[40,2,64,128]{3,2,1,0:T(8,128)(2,1)S(1)}, u32[]{:S(2)}, u32[]{:S(2)}) collective-permute-start(bf16[40,2,64,128]{3,2,1,0:T(8,128)(2,1)} %gather_blocks.3), channel_id=1, source_target_pairs={{0,1},{1,0},{2,3},{3,2},{4,5},{5,4},{6,7},{7,6},{8,9},{9,8},{10,11... | collective-permute-start | bytes 3932168 | tf_op jit(solution)/shard_map/ppermute | solution.py:299
  149.1 13.2 %collective-permute-start.11 = (bf16[30,2,64,128]{3,2,1,0:T(8,128)(2,1)}, bf16[30,2,64,128]{3,2,1,0:T(8,128)(2,1)}, u32[]{:S(2)}, u32[]{:S(2)}) collective-permute-start(bf16[30,2,64,128]{3,2,1,0:T(8,128)(2,1)} %copy-done.1), channel_id=1, source_target_pairs={{0,6},{8,14},{16,22},{24,30},{1,7},{9,15},{17,23},{25,31}} | collective-permute-start | bytes 2949128 | tf_op jit(solution)/shard_map/ppermute | solution.py:297
  151.4 21.4 %collective-permute-start.8 = (bf16[30,2,64,128]{3,2,1,0:T(8,128)(2,1)}, bf16[30,2,64,128]{3,2,1,0:T(8,128)(2,1)}, u32[]{:S(2)}, u32[]{:S(2)}) collective-permute-start(bf16[30,2,64,128]{3,2,1,0:T(8,128)(2,1)} %collective-permute-done.2.refs_3_), channel_id=1, source_target_pairs={{0,6},{8,14},{16,22},{24,30},{1,7},{9,15},{17,23},{25,31}} | collective-permute-start | bytes 2949128 | tf_op jit(solution)/shard_map/ppermute | solution.py:297
  153.6 29.7 %collective-permute-start.9 = (bf16[30,2,64,128]{3,2,1,0:T(8,128)(2,1)}, bf16[30,2,64,128]{3,2,1,0:T(8,128)(2,1)}, u32[]{:S(2)}, u32[]{:S(2)}) collective-permute-start(bf16[30,2,64,128]{3,2,1,0:T(8,128)(2,1)} %collective-permute-done.3.refs_4_), channel_id=1, source_target_pairs={{0,6},{8,14},{16,22},{24,30},{1,7},{9,15},{17,23},{25,31}} | collective-permute-start | bytes 2949128 | tf_op jit(solution)/shard_map/ppermute | solution.py:297
  183.4 2.1 copy-start
  185.5 1.2 copy-start.2
  207.4 5.0 %collective-permute-start.14 = (f32[4,2,32,64]{3,2,1,0:T(8,128)S(1)}, f32[4,2,32,64]{3,2,1,0:T(8,128)S(1)}, u32[]{:S(2)}, u32[]{:S(2)}) collective-permute-start(f32[4,2,32,64]{3,2,1,0:T(8,128)S(1)} %slice_select_fusion), channel_id=1, source_target_pairs={{0,1},{1,0},{2,3},{3,2},{4,5},{5,4},{6,7},{7,6},{8,9},{9,8},{10,11... | collective-permute-start | bytes 196616 | tf_op jit(solution)/shard_map/ppermute | solution.py:307
  212.5 32.1 %collective-permute-start.15 = (f32[2,2,32,64]{3,2,1,0:T(8,128)S(1)}, f32[2,2,32,64]{3,2,1,0:T(8,128)S(1)}, u32[]{:S(2)}, u32[]{:S(2)}) collective-permute-start(f32[2,2,32,64]{3,2,1,0:T(8,128)S(1)} %slice.102), channel_id=1, source_target_pairs={{8,0},{10,2},{12,4},{14,6},{16,8},{18,10},{20,12},{22,14},{24,16},... | collective-permute-start | bytes 98312 | tf_op jit(solution)/shard_map/ppermute | solution.py:308
  244.6 5.8 %collective-permute-start.16 = (f32[2,32,64]{2,1,0:T(8,128)S(1)}, f32[2,32,64]{2,1,0:T(8,128)S(1)}, u32[]{:S(2)}, u32[]{:S(2)}) collective-permute-start(f32[2,32,64]{2,1,0:T(8,128)S(1)} %get-tuple-element.22), channel_id=1, source_target_pairs={{24,0},{26,2},{28,4},{30,6},{0,8},{2,10},{4,12},{6,14},{8,16},{10,... | collective-permute-start | bytes 49160 | tf_op jit(solution)/shard_map/ppermute | solution.py:309

commit v2 on v0

--- a/solution.py
+++ b/solution.py
@@ -1,7 +1,13 @@
+import functools
+
 import jax
 import jax.numpy as jnp
 from jax import lax
 from jax.sharding import PartitionSpec as P
+from jax.experimental import pallas as pl
+from jax.experimental.pallas import tpu as pltpu
+
+CHUNKS = 4
 
 
 def shifted(block, axis, distance):
@@ -122,9 +128,341 @@
     return lax.dynamic_slice_in_dim(total, my_slice * row_count, row_count, 3)
 
 
+def gather_kernel(count, index_ref, source_ref, out_ref, sems):
+    def copy(i):
+        return pltpu.make_async_copy(source_ref.at[index_ref[i]], out_ref.at[i], sems.at[i])
+
+    def begin(i, carry):
+        copy(i).start()
+        return carry
+
+    def finish(i, carry):
+        copy(i).wait()
+        return carry
+
+    lax.fori_loop(0, count, begin, 0)
+    lax.fori_loop(0, count, finish, 0)
+
+
+def gather_blocks(index, source):
+    count = index.shape[0]
+    shape = (count,) + source.shape[1:]
+    return pl.pallas_call(
+        functools.partial(gather_kernel, count),
+        out_shape=jax.ShapeDtypeStruct(shape, source.dtype),
+        in_specs=[
+            pl.BlockSpec(memory_space=pltpu.SMEM),
+            pl.BlockSpec(memory_space=pl.ANY),
+        ],
+        out_specs=pl.BlockSpec(memory_space=pltpu.VMEM),
+        scratch_shapes=[pltpu.SemaphoreType.DMA((count,))],
+        name="gather_blocks",
+        cost_estimate=pl.CostEstimate(flops=0, bytes_accessed=4 * source.dtype.itemsize * count * source[0].size, transcendentals=0),
+    )(index, source)
+
+
+def plan_kernel(slab, capacity, shift_ref, map_ref, local_ref, sent_ref, got_ref):
+    mine = lax.axis_index("ga")
+    base = mine * slab
+    for e in range(4):
+        shift = shift_ref[e]
+
+        def here(j, counts):
+            own, out = counts
+            source = map_ref[shift, base + j] - base
+            inside = (source >= 0) & (source < slab)
+            local_ref[0, e, own] = j
+            local_ref[1, e, own] = source
+            sent_ref[e, out] = j
+            return own + inside.astype(jnp.int32), out + 1 - inside.astype(jnp.int32)
+
+        def there(j, count):
+            source = map_ref[shift, slab - base + j] - base
+            inside = (source >= 0) & (source < slab)
+            got_ref[e, count] = source
+            return count + inside.astype(jnp.int32)
+
+        lax.fori_loop(0, slab, here, (jnp.int32(0), jnp.int32(0)), unroll=8)
+        lax.fori_loop(0, slab, there, jnp.int32(0), unroll=8)
+
+
+def plan(shifts, block_map, slab, capacity):
+    own_count = slab - capacity
+    return pl.pallas_call(
+        functools.partial(plan_kernel, slab, capacity),
+        out_shape=(
+            jax.ShapeDtypeStruct((2, 4, own_count + 8), jnp.int32),
+            jax.ShapeDtypeStruct((4, capacity + 8), jnp.int32),
+            jax.ShapeDtypeStruct((4, capacity + 8), jnp.int32),
+        ),
+        in_specs=[pl.BlockSpec(memory_space=pltpu.SMEM)] * 2,
+        out_specs=[pl.BlockSpec(memory_space=pltpu.SMEM)] * 3,
+        name="plan",
+    )(shifts, block_map)
+
+
+def meet_kernel(
+    points, slab, capacity, local_ref, other_ref, send_ref, own_hbm, mine_out, out_ref,
+    own, upper, lower, nxt, got_own, lower_out, got_lower, local_sems, send_sems, recv_sems,
+):
+    row = points // 4
+    me = lax.axis_index("ka")
+    partner = 1 - lax.axis_index("ga")
+    z, column = me // row, me % row
+    even = column % 2 == 0
+    middle = (z == 1) | (z == 2)
+    holds_pair = (even & ~middle) | (~even & middle)
+    below = {"ka": (me + points - row) % points}
+    above = {"ka": (me + row) % points}
+    left = {"ka": z * row + (column + row - 1) % row}
+    right = {"ka": z * row + (column + 1) % row}
+    across = {"ga": partner}
+    bands, lanes = own.shape[2], own.shape[3]
+    size = slab // CHUNKS
+    own_count = slab - capacity
+
+    barrier = pltpu.get_barrier_semaphore()
+    for peer in (below, above, left, right, across):
+        pl.semaphore_signal(barrier, inc=1, device_id=peer, device_id_type=pl.DeviceIdType.MESH)
+    pl.semaphore_wait(barrier, 5)
+
+    def remote(source, target, n, peer):
+        return pltpu.make_async_remote_copy(
+            src_ref=source, dst_ref=target, send_sem=send_sems.at[n], recv_sem=recv_sems.at[n],
+            device_id=peer, device_id_type=pl.DeviceIdType.MESH,
+        )
+
+    def chunk(c):
+        return pl.ds(c * size, size)
+
+    keep = pltpu.make_async_copy(own_hbm, own, local_sems.at[0])
+    swap_own = remote(mine_out, got_own, 0, across)
+    swap_lower = remote(lower_out, got_lower, 1, across)
+    rise = [remote(own_hbm.at[chunk(c)], lower.at[chunk(c)], 2 + c, above) for c in range(CHUNKS)]
+    fall = [remote(own_hbm.at[chunk(c)], upper.at[chunk(c)], 2 + CHUNKS + c, below) for c in range(CHUNKS)]
+    pass_own = [remote(own_hbm.at[chunk(c)], nxt.at[chunk(c)], 2 + 2 * CHUNKS + c, left) for c in range(CHUNKS)]
+    pass_on = [remote(upper.at[chunk(c)], nxt.at[chunk(c)], 2 + 2 * CHUNKS + c, left) for c in range(CHUNKS)]
+
+    falls = even | (z >= 2)
+    rises = ~even | (z >= 2)
+    gets_upper = even | middle
+    gets_lower = ~even | ~middle
+
+    @pl.when(falls)
+    def _():
+        for copy in fall:
+            copy.start()
+
+    @pl.when(rises)
+    def _():
+        for copy in rise:
+            copy.start()
+
+    @pl.when(column > 0)
+    def _():
+        for copy in pass_own:
+            copy.start()
+
+    swap_own.start()
+    keep.start()
+
+    def pick(ref, at):
+        return ref[at].reshape(2 * bands, lanes)
+
+    def product(total, first_left, second_left, first_right, second_right):
+        return total + lax.dot_general(
+            jnp.concatenate([first_left, second_left], axis=1),
+            jnp.concatenate([first_right, second_right], axis=1),
+            (((1,), (1,)), ((), ())),
+            preferred_element_type=jnp.float32,
+        )
+
+    def edge(e, bra, ket, got, got_at, bra_sent):
+        def own_step(i, total):
+            for u in range(0, 10, 2):
+                n = i * 10 + u
+                total = product(
+                    total,
+                    pick(bra, local_ref[0, e, n]), pick(bra, local_ref[0, e, n + 1]),
+                    pick(ket, local_ref[1, e, n]), pick(ket, local_ref[1, e, n + 1]),
+                )
+            return total
+
+        def cross_step(i, total):
+            n = i * 2
+            travelled = pick(got, got_at + n), pick(got, got_at + n + 1)
+            stayed_ref = ket if bra_sent else bra
+            stayed = pick(stayed_ref, other_ref[e, n]), pick(stayed_ref, other_ref[e, n + 1])
+            if bra_sent:
+                return product(total, *travelled, *stayed)
+            return product(total, *stayed, *travelled)
+
+        total = jnp.zeros((2 * bands, 2 * bands), jnp.float32)
+        total = lax.fori_loop(0, own_count // 10, own_step, total)
+        total = lax.fori_loop(0, capacity // 2, cross_step, total)
+        out_ref[e, 0] = total[:bands, :bands] + total[bands:, bands:]
+        out_ref[e, 1] = total[:bands, bands:] - total[bands:, :bands]
+
+    keep.wait()
+    swap_own.wait_recv()
+
+    def next_edge():
+        for copy in pass_own:
+            copy.wait_recv()
+        edge(0, own, nxt, got_own, 0, True)
+
+    @pl.when(column < row - 1)
+    def _():
+        next_edge()
+
+    @pl.when(gets_upper)
+    def _():
+        for copy, onward in zip(fall, pass_on):
+            copy.wait_recv()
+
+            @pl.when(column == 0)
+            def _():
+                onward.start()
+
+    @pl.when(gets_lower)
+    def _():
+        for copy in rise:
+            copy.wait_recv()
+
+    @pl.when(holds_pair)
+    def _():
+        def gather(r, carry):
+            lower_out[r] = lower[send_ref[r]]
+            return carry
+
+        lax.fori_loop(0, 2 * capacity, gather, 0)
+        swap_lower.start()
+
+    @pl.when(even)
+    def _():
+        edge(1, own, upper, got_own, capacity, True)
+
+    @pl.when(~even)
+    def _():
+        edge(1, lower, own, got_own, capacity, False)
+
+    @pl.when(column == row - 1)
+    def _():
+        next_edge()
+
+    @pl.when(holds_pair)
+    def _():
+        swap_lower.wait_recv()
+        edge(2, lower, upper, got_lower, 0, True)
+        edge(3, upper, lower, got_lower, capacity, False)
+        swap_lower.wait_send()
+
+    @pl.when(~holds_pair)
+    def _():
+        out_ref[2] = jnp.zeros_like(out_ref[2])
+        out_ref[3] = jnp.zeros_like(out_ref[3])
+
+    swap_own.wait_send()
+
+    @pl.when(falls)
+    def _():
+        for copy in fall:
+            copy.wait_send()
+
+    @pl.when(rises)
+    def _():
+        for copy in rise:
+            copy.wait_send()
+
+    @pl.when(column > 0)
+    def _():
+        for copy in pass_own:
+            copy.wait_send()
+
+    @pl.when(column == 0)
+    def _():
+        for copy in pass_on:
+            copy.wait_send()
+
+
+def meet(local, other, send, own, mine_out, points, capacity):
+    slab, bands = own.shape[0], own.shape[2]
+    block = own.shape[1:]
+    copies = 2 + 3 * CHUNKS
+    return pl.pallas_call(
+        functools.partial(meet_kernel, points, slab, capacity),
+        out_shape=jax.ShapeDtypeStruct((4, 2, bands, bands), jnp.float32),
+        in_specs=[pl.BlockSpec(memory_space=pltpu.SMEM)] * 3 + [pl.BlockSpec(memory_space=pl.ANY)] * 2,
+        out_specs=pl.BlockSpec(memory_space=pltpu.VMEM),
+        scratch_shapes=[pltpu.VMEM((slab,) + block, own.dtype)] * 4
+        + [pltpu.VMEM((2 * capacity,) + block, own.dtype)] * 3
+        + [pltpu.SemaphoreType.DMA((1,)), pltpu.SemaphoreType.DMA((copies,)), pltpu.SemaphoreType.DMA((copies,))],
+        compiler_params=pltpu.CompilerParams(
+            collective_id=0, has_side_effects=True, vmem_limit_bytes=32 * 2**20
+        ),
+        name="meet",
+    )(local, other, send, own, mine_out)
+
+
+def on_four_rows(coeffs, neighbour, shift_id, block_map):
+    own = coeffs[0]
+    slab = own.shape[0]
+    points = lax.axis_size("ka")
+    row = points // 4
+    me = lax.axis_index("ka")
+    first = lax.axis_index("ga") == 0
+    even = jnp.mod(jnp.mod(me, row), 2) == 0
+    capacity = 2 * max(1, slab // 12)
+    to_lower = [((k + row) % points, k) for k in range(points)]
+    to_upper = [((k - row) % points, k) for k in range(points)]
+    swap = [(0, 1), (1, 0)]
+
+    def role_shift(step):
+        return jnp.sum(jnp.where(neighbour[0] == jnp.mod(me + step, points), shift_id[0], 0))
+
+    row_shift, half_shift = role_shift(row), role_shift(points // 2)
+    sent = jnp.stack([row_shift, half_shift])
+    lower = lax.ppermute(sent, "ka", to_upper)
+    upper = lax.ppermute(sent, "ka", to_lower)
+    shifts = jnp.stack([role_shift(1), jnp.where(even, row_shift, lower[0]), lower[1], upper[1]])
+
+    local, bras, kets = plan(shifts, block_map, slab, capacity)
+    bras, kets = bras[:, :capacity], kets[:, :capacity]
+    sends_bra = jnp.stack([even | True, even, even | True, even & False])[:, None]
+    send = jnp.where(sends_bra, bras, kets)
+    other = jnp.where(sends_bra, kets, bras)
+    mine_out = gather_blocks(send[:2].reshape(-1), own)
+    sums = meet(local, other, send[2:].reshape(-1), own, mine_out, points, capacity)
+
+    half = sums.shape[2] // 2
+    low_rows, high_rows = sums[:, :, :half], sums[:, :, half:]
+    kept = jnp.where(first, low_rows, high_rows)
+    total = kept + lax.ppermute(jnp.where(first, high_rows, low_rows), "ga", swap)
+    from_upper = lax.ppermute(total[1:3], "ka", to_lower)
+    from_lower = lax.ppermute(total[3], "ka", to_upper)
+    row_sum = jnp.where(even, total[1], from_upper[0])
+    half_sum = from_upper[1] + from_lower
+    target = neighbour[0][:, None, None, None]
+    out = jnp.where(
+        target == jnp.mod(me + 1, points),
+        total[0],
+        jnp.where(target == jnp.mod(me + row, points), row_sum, half_sum),
+    )
+    return out[None]
+
+
 def solution(mesh):
     in_specs = (P("ka", "ga", None, None, None), P("ka", None), P("ka", None), P())
     out_specs = P("ka", None, None, "ga", None)
-    return jax.shard_map(
-        on_device, mesh=mesh, in_specs=in_specs, out_specs=out_specs, check_vma=False
-    )
+    four_rows = mesh.shape["ga"] == 2 and mesh.shape["ka"] == 4 * min(16, mesh.shape["ka"] // 4)
+
+    def run(coeffs, neighbour, shift_id, block_map):
+        one_each = coeffs.shape[0] == mesh.shape["ka"]
+        per_slice = coeffs.shape[1] // mesh.shape["ga"]
+        whole_chunks = per_slice % (2 * CHUNKS) == 0 or per_slice % CHUNKS == 0 and per_slice % 2 == 0
+        body = on_four_rows if four_rows and one_each and whole_chunks else on_device
+        return jax.shard_map(
+            body, mesh=mesh, in_specs=in_specs, out_specs=out_specs, check_vma=False
+        )(coeffs, neighbour, shift_id, block_map)
+
+    return run

time: 408 us -> 252 us (0.62)
  waiting for transfers between devices: 281 us -> 19.7 us
  Pallas kernels: 0 us -> 212 us
  local copies, waits for them, and re-layouts: 64.7 us -> 5.42 us
  other arithmetic: 21 us -> 6.92 us
  starting transfers between devices: 18.1 us -> 5.78 us
  between operations: 13.6 us -> 1.35 us
  matrix products: 9.31 us -> 0 us
    pallas_call x0 -> x3, Pallas kernels: none -> 212 us  [the longest x1 200 us: meet(): pl.pallas_call(functools.partial(meet_kernel, points, slab, capacity), ou...]
    ppermute x3 -> x5, waiting for transfers between devices: 214 us -> 19.7 us  [the longest x1 5.7 us: on_four_rows(): from_lower = lax.ppermute(total[3], 'ka', to_upper)]
    gather x6 -> x0, local copies, waits for them, and re-layouts: 54.4 us -> none  [the longest x2 32 us: on_device(): ket_self = kets[ket_index[:, None], self_place]]
    all_to_all x3 -> x0, waiting for transfers between devices: 43.7 us -> none  [the longest x1 43.7 us: on_device(): lax.all_to_all(payload, 'ga', split_axis=1, concat_axis=1, tiled=True)]
    psum x1 -> x0, waiting for transfers between devices: 22.9 us -> none  [on_device(): total = lax.psum(summed_part, 'ga')]
    concatenate x6 -> x0, other arithmetic: 13.6 us -> none  [the longest x1 12.7 us: on_device(): jnp.concatenate([coeffs, row_point, plane_kets, opposite], axis=0)]
    all_to_all x3 -> x0, starting transfers between devices: 11.9 us -> none  [the longest x1 5.5 us: on_device(): lax.all_to_all(payload, 'ga', split_axis=1, concat_axis=1, tiled=True)]
    dot_general x8 -> x0, matrix products: 9.31 us -> none  [the longest x2 2.37 us: complex_intersection(): jnp.einsum(form, bra_real, ket_real, preferred_element_type=jnp.float32)]
  transfers between devices with their start and end apart: 7 -> 5, of which waited for: 5 -> 4; matrix products, arithmetic and copies ran while one was open for 6% -> 0% of each run, Pallas kernels for 0% -> 0%
where the time goes in v2:
time: 252 us; the launch traced here: 251 us
  Pallas kernels  212 us (84%)
  waiting for transfers between devices  19.7 us (8%)
  other arithmetic  6.92 us (3%)
  starting transfers between devices  5.78 us (2%)
  local copies, waits for them, and re-layouts  5.42 us (2%)
    pallas_call x1, Pallas kernels, meet(): pl.pallas_call(functools.partial(meet_kernel, points, slab, capacity), ou...  200 us
    pallas_call x1, Pallas kernels, plan(): pl.pallas_call(functools.partial(plan_kernel, slab, capacity), out_shape=...  8.9 us
    ppermute x1, waiting for transfers between devices, on_four_rows(): from_lower = lax.ppermute(total[3], 'ka', to_upper)  5.7 us
    ppermute x1, waiting for transfers between devices, on_four_rows(): lower = lax.ppermute(sent, 'ka', to_upper)  5.28 us
    ppermute x1, starting transfers between devices, on_four_rows(): upper = lax.ppermute(sent, 'ka', to_lower)  5.08 us
  transfers between devices with their start and end apart: 5, of which 4 were waited for; matrix products, arithmetic and copies ran while one was open for 0% of the time, Pallas kernels for 0%

profile of v2, /device:TPU:0, one launch (start us, length us, event | category | flops | bytes accessed | tf_op | source)
XLA Modules:
  0.0 251.4 jit_solution(10039161488252507254)
XLA Ops:
  0.0 1.4 fusion.3
  1.4 1.3 pad_add_fusion.1
  2.7 5.1 %collective-permute-start.1 = (s32[2]{0:T(128)S(1)}, s32[2]{0:T(128)S(1)}, u32[]{:S(2)}, u32[]{:S(2)}) collective-permute-start(s32[2]{0:T(128)S(1)} %pad_add_fusion.1), channel_id=1, source_target_pairs={{8,0},{10,2},{12,4},{14,6},{16,8},{18,10},{20,12},{22,14},{24,16},... | collective-permute-start | bytes 32 | tf_op jit(solution)/shard_map/ppermute | solution.py:426
  7.8 0.0 collective-permute-start
  7.8 0.1 pad_add_fusion
  7.9 5.3 %collective-permute-done = s32[2]{0:T(128)S(1)} collective-permute-done((s32[2]{0:T(128)S(1)}, s32[2]{0:T(128)S(1)}, u32[]{:S(2)}, u32[]{:S(2)}) %collective-permute-start) | collective-permute-done | bytes 40 | tf_op jit(solution)/shard_map/ppermute | solution.py:425
  13.2 0.7 fusion.6
  15.1 0.0 collective-permute-done.1
  15.1 0.6 slice.47
  15.7 2.5 %pad_add_fusion.2.shift_ref = s32[4]{0:T(128)} fusion(s32[1]{0:T(128)} %slice.47, s32[1]{0:T(128)} %get-tuple-element.24, s32[1]{0:T(128)} %bitcast.8, s32[1]{0:T(128)} %bitcast.2), kind=kLoop, calls=%fused_computation.17 | loop fusion | flops 12 | bytes 32 | tf_op jit(solution)/shard_map/stack | solution.py:427
  18.2 8.9 %plan.1 = (s32[2,4,108]{2,1,0:T(4,128)}, s32[4,28]{1,0:T(4,128)}, s32[4,28]{1,0:T(4,128)}) custom-call(s32[4]{0:T(128)} %pad_add_fusion.2.shift_ref, s32[8,240]{1,0:T(8,128)} %map_ref.1), custom_call_target="tpu_custom_call" | custom-call | tf_op jit(solution)/shard_map/plan/pallas_call | solution.py:191
  27.1 0.0 copy-start.2
  27.2 0.8 slice_select_fusion.2
  27.9 0.7 reshape.36.index_ref
  28.6 0.1 reshape.35.send_ref
  28.7 3.4 %gather_blocks.1.mine_out = bf16[40,2,64,128]{3,2,1,0:T(8,128)(2,1)} custom-call(s32[40]{0:T(128)} %reshape.36.index_ref, bf16[120,2,64,128]{3,2,1,0:T(8,128)(2,1)} %bitcast.35), custom_call_target="tpu_custom_call" | custom-call | bytes 5242880 | tf_op jit(solution)/shard_map/gather_blocks/pallas_call | solution.py:150
  32.0 0.0 copy-done.2
  32.1 0.0 copy-start
  32.1 2.1 copy-done
  34.2 0.0 copy-start.1
  34.2 1.3 copy-done.1
  35.5 199.9 %meet.1 = f32[4,2,64,64]{3,2,1,0:T(8,128)S(1)} custom-call(s32[2,4,108]{2,1,0:T(4,128)S(1)} %copy-done.2, s32[4,20]{1,0:T(4,128)S(1)} %get-tuple-element.20.other_ref, s32[40]{0:T(128)S(1)} %reshape.35.send_ref, bf16[120,2,64,128]{3,2,1,0:T(8,128)(2,1)S(1)} %bitcast.36, bf16[40,2,64,128]{3,2,1,0:T(8,128)(2,1)S(1)} %copy-done.1), custom_call_target="tpu_custom_call" | custom-call | tf_op jit(solution)/shard_map/meet/pallas_call | solution.py:392
  235.5 0.6 collective-permute-start.2
  236.0 4.4 %collective-permute-done.2 = f32[4,2,32,64]{3,2,1,0:T(8,128)S(1)} collective-permute-done((f32[4,2,32,64]{3,2,1,0:T(8,128)S(1)}, f32[4,2,32,64]{3,2,1,0:T(8,128)S(1)}, u32[]{:S(2)}, u32[]{:S(2)}) %collective-permute-start.2) | collective-permute-done | bytes 65568 | tf_op jit(solution)/shard_map/ppermute | solution.py:440
  240.5 0.1 collective-permute-start.3
  240.6 4.3 %collective-permute-done.3 = f32[2,2,32,64]{3,2,1,0:T(8,128)S(1)} collective-permute-done((f32[2,2,32,64]{3,2,1,0:T(8,128)S(1)}, f32[2,2,32,64]{3,2,1,0:T(8,128)S(1)}, u32[]{:S(2)}, u32[]{:S(2)}) %collective-permute-start.3) | collective-permute-done | bytes 32800 | tf_op jit(solution)/shard_map/ppermute | solution.py:441
  244.9 0.1 collective-permute-start.4
  244.9 5.7 %collective-permute-done.4 = f32[2,32,64]{2,1,0:T(8,128)S(1)} collective-permute-done((f32[2,32,64]{2,1,0:T(8,128)S(1)}, f32[2,32,64]{2,1,0:T(8,128)S(1)}, u32[]{:S(2)}, u32[]{:S(2)}) %collective-permute-start.4) | collective-permute-done | bytes 16416 | tf_op jit(solution)/shard_map/ppermute | solution.py:442
  250.6 0.7 select_select_fusion
  (6 shorter events, 0.1 us)
Async XLA Ops:
  2.7 12.4 %collective-permute-start.1 = (s32[2]{0:T(128)S(1)}, s32[2]{0:T(128)S(1)}, u32[]{:S(2)}, u32[]{:S(2)}) collective-permute-start(s32[2]{0:T(128)S(1)} %pad_add_fusion.1), channel_id=1, source_target_pairs={{8,0},{10,2},{12,4},{14,6},{16,8},{18,10},{20,12},{22,14},{24,16},... | collective-permute-start | bytes 32 | tf_op jit(solution)/shard_map/ppermute | solution.py:426
  7.8 5.4 %collective-permute-start = (s32[2]{0:T(128)S(1)}, s32[2]{0:T(128)S(1)}, u32[]{:S(2)}, u32[]{:S(2)}) collective-permute-start(s32[2]{0:T(128)S(1)} %pad_add_fusion.1), channel_id=1, source_target_pairs={{24,0},{26,2},{28,4},{30,6},{0,8},{2,10},{4,12},{6,14},{8,16},{10,... | collective-permute-start | bytes 32 | tf_op jit(solution)/shard_map/ppermute | solution.py:425
  27.1 4.9 %copy-start.2 = (s32[2,4,108]{2,1,0:T(4,128)S(1)}, s32[2,4,108]{2,1,0:T(4,128)}, u32[]{:S(2)}) copy-start(s32[2,4,108]{2,1,0:T(4,128)} %get-tuple-element.8.local_ref) | copy-start | bytes 10372
  32.1 2.1 copy-start
  34.2 1.3 copy-start.1
  235.5 5.0 %collective-permute-start.2 = (f32[4,2,32,64]{3,2,1,0:T(8,128)S(1)}, f32[4,2,32,64]{3,2,1,0:T(8,128)S(1)}, u32[]{:S(2)}, u32[]{:S(2)}) collective-permute-start(f32[4,2,32,64]{3,2,1,0:T(8,128)S(1)} %slice_select_fusion), channel_id=1, source_target_pairs={{0,1},{1,0},{2,3},{3,2},{4,5},{5,4},{6,7},{7,6},{8,9},{9,8},{10,11... | collective-permute-start | bytes 196616 | tf_op jit(solution)/shard_map/ppermute | solution.py:440
  240.5 4.3 %collective-permute-start.3 = (f32[2,2,32,64]{3,2,1,0:T(8,128)S(1)}, f32[2,2,32,64]{3,2,1,0:T(8,128)S(1)}, u32[]{:S(2)}, u32[]{:S(2)}) collective-permute-start(f32[2,2,32,64]{3,2,1,0:T(8,128)S(1)} %slice.62), channel_id=1, source_target_pairs={{8,0},{10,2},{12,4},{14,6},{16,8},{18,10},{20,12},{22,14},{24,16},... | collective-permute-start | bytes 98312 | tf_op jit(solution)/shard_map/ppermute | solution.py:441
  244.9 5.8 %collective-permute-start.4 = (f32[2,32,64]{2,1,0:T(8,128)S(1)}, f32[2,32,64]{2,1,0:T(8,128)S(1)}, u32[]{:S(2)}, u32[]{:S(2)}) collective-permute-start(f32[2,32,64]{2,1,0:T(8,128)S(1)} %get-tuple-element.17), channel_id=1, source_target_pairs={{24,0},{26,2},{28,4},{30,6},{0,8},{2,10},{4,12},{6,14},{8,16},{10,... | collective-permute-start | bytes 49160 | tf_op jit(solution)/shard_map/ppermute | solution.py:442

commit v3 on v2

--- a/solution.py
+++ b/solution.py
@@ -211,7 +211,7 @@
     z, column = me // row, me % row
     even = column % 2 == 0
     middle = (z == 1) | (z == 2)
-    holds_pair = (even & ~middle) | (~even & middle)
+    holds_pair = middle
     below = {"ka": (me + points - row) % points}
     above = {"ka": (me + row) % points}
     left = {"ka": z * row + (column + row - 1) % row}
@@ -244,27 +244,25 @@
     pass_on = [remote(upper.at[chunk(c)], nxt.at[chunk(c)], 2 + 2 * CHUNKS + c, left) for c in range(CHUNKS)]
 
     falls = even | (z >= 2)
-    rises = ~even | (z >= 2)
+    rises = ~even | (z <= 1)
     gets_upper = even | middle
-    gets_lower = ~even | ~middle
-
-    @pl.when(falls)
-    def _():
-        for copy in fall:
-            copy.start()
-
-    @pl.when(rises)
-    def _():
-        for copy in rise:
-            copy.start()
-
-    @pl.when(column > 0)
-    def _():
-        for copy in pass_own:
-            copy.start()
-
+    gets_lower = ~even | middle
+
+    keep.start()
     swap_own.start()
-    keep.start()
+    for c in range(CHUNKS):
+
+        @pl.when(column > 0)
+        def _():
+            pass_own[c].start()
+
+        @pl.when(falls)
+        def _():
+            fall[c].start()
+
+        @pl.when(rises)
+        def _():
+            rise[c].start()
 
     def pick(ref, at):
         return ref[at].reshape(2 * bands, lanes)

time: 252 us -> 214 us (0.85)
  Pallas kernels: 212 us -> 142 us
  waiting for transfers between devices: 19.7 us -> 38.1 us
  starting transfers between devices: 5.78 us -> 20.2 us
    pallas_call x1, Pallas kernels: 200 us -> 130 us  [meet(): pl.pallas_call(functools.partial(meet_kernel, points, slab, capacity), ou...]
    ppermute x1, waiting for transfers between devices: 4.25 us -> 26.5 us  [on_four_rows(): from_upper = lax.ppermute(total[1:3], 'ka', to_lower)]
    ppermute x1, starting transfers between devices: 0.06 us -> 8.45 us  [on_four_rows(): from_lower = lax.ppermute(total[3], 'ka', to_upper)]
    ppermute x1, starting transfers between devices: 0.06 us -> 5.46 us  [on_four_rows(): from_upper = lax.ppermute(total[1:3], 'ka', to_lower)]
    ppermute x1, waiting for transfers between devices: 5.7 us -> 2.45 us  [on_four_rows(): from_lower = lax.ppermute(total[3], 'ka', to_upper)]
where the time goes in v3:
time: 214 us
  Pallas kernels  142 us (66%)
  waiting for transfers between devices  38.1 us (18%)
  starting transfers between devices  20.2 us (9%)
  other arithmetic  6.92 us (3%)
  local copies, waits for them, and re-layouts  5.42 us (3%)
    pallas_call x1, Pallas kernels, meet(): pl.pallas_call(functools.partial(meet_kernel, points, slab, capacity), ou...  130 us
    ppermute x1, waiting for transfers between devices, on_four_rows(): from_upper = lax.ppermute(total[1:3], 'ka', to_lower)  26.5 us
    pallas_call x1, Pallas kernels, plan(): pl.pallas_call(functools.partial(plan_kernel, slab, capacity), out_shape=...  8.9 us
    ppermute x1, starting transfers between devices, on_four_rows(): from_lower = lax.ppermute(total[3], 'ka', to_upper)  8.45 us
    ppermute x1, starting transfers between devices, on_four_rows(): from_upper = lax.ppermute(total[1:3], 'ka', to_lower)  5.46 us
    ppermute x1, waiting for transfers between devices, on_four_rows(): lower = lax.ppermute(sent, 'ka', to_upper)  5.28 us
    ppermute x1, starting transfers between devices, on_four_rows(): upper = lax.ppermute(sent, 'ka', to_lower)  5.08 us
  transfers between devices with their start and end apart: 5, of which 4 were waited for; matrix products, arithmetic and copies ran while one was open for 0% of the time, Pallas kernels for 0%

profile of v3, /device:TPU:0, one launch (start us, length us, event | category | flops | bytes accessed | tf_op | source)
XLA Modules:
  0.0 213.9 jit_solution(12529448222589747822)
XLA Ops:
  0.0 1.4 fusion.3
  1.4 1.3 pad_add_fusion.1
  2.7 5.1 %collective-permute-start.1 = (s32[2]{0:T(128)S(1)}, s32[2]{0:T(128)S(1)}, u32[]{:S(2)}, u32[]{:S(2)}) collective-permute-start(s32[2]{0:T(128)S(1)} %pad_add_fusion.1), channel_id=1, source_target_pairs={{8,0},{10,2},{12,4},{14,6},{16,8},{18,10},{20,12},{22,14},{24,16},... | collective-permute-start | bytes 32 | tf_op jit(solution)/shard_map/ppermute | solution.py:424
  7.8 0.0 collective-permute-start
  7.8 0.1 pad_add_fusion
  7.9 5.3 %collective-permute-done = s32[2]{0:T(128)S(1)} collective-permute-done((s32[2]{0:T(128)S(1)}, s32[2]{0:T(128)S(1)}, u32[]{:S(2)}, u32[]{:S(2)}) %collective-permute-start) | collective-permute-done | bytes 40 | tf_op jit(solution)/shard_map/ppermute | solution.py:423
  13.2 0.7 fusion.6
  15.1 0.0 collective-permute-done.1
  15.1 0.6 slice.47
  15.7 2.5 %pad_add_fusion.2.shift_ref = s32[4]{0:T(128)} fusion(s32[1]{0:T(128)} %slice.47, s32[1]{0:T(128)} %get-tuple-element.24, s32[1]{0:T(128)} %bitcast.8, s32[1]{0:T(128)} %bitcast.2), kind=kLoop, calls=%fused_computation.17 | loop fusion | flops 12 | bytes 32 | tf_op jit(solution)/shard_map/stack | solution.py:425
  18.2 8.9 %plan.1 = (s32[2,4,108]{2,1,0:T(4,128)}, s32[4,28]{1,0:T(4,128)}, s32[4,28]{1,0:T(4,128)}) custom-call(s32[4]{0:T(128)} %pad_add_fusion.2.shift_ref, s32[8,240]{1,0:T(8,128)} %map_ref.1), custom_call_target="tpu_custom_call" | custom-call | tf_op jit(solution)/shard_map/plan/pallas_call | solution.py:191
  27.1 0.0 copy-start.2
  27.2 0.8 slice_select_fusion.2
  27.9 0.7 reshape.36.index_ref
  28.6 0.1 reshape.35.send_ref
  28.7 3.4 %gather_blocks.1.mine_out = bf16[40,2,64,128]{3,2,1,0:T(8,128)(2,1)} custom-call(s32[40]{0:T(128)} %reshape.36.index_ref, bf16[120,2,64,128]{3,2,1,0:T(8,128)(2,1)} %bitcast.35), custom_call_target="tpu_custom_call" | custom-call | bytes 5242880 | tf_op jit(solution)/shard_map/gather_blocks/pallas_call | solution.py:150
  32.0 0.0 copy-done.2
  32.1 0.0 copy-start
  32.1 2.1 copy-done
  34.2 0.0 copy-start.1
  34.2 1.3 copy-done.1
  35.5 129.7 %meet.1 = f32[4,2,64,64]{3,2,1,0:T(8,128)S(1)} custom-call(s32[2,4,108]{2,1,0:T(4,128)S(1)} %copy-done.2, s32[4,20]{1,0:T(4,128)S(1)} %get-tuple-element.20.other_ref, s32[40]{0:T(128)S(1)} %reshape.35.send_ref, bf16[120,2,64,128]{3,2,1,0:T(8,128)(2,1)S(1)} %bitcast.36, bf16[40,2,64,128]{3,2,1,0:T(8,128)(2,1)S(1)} %copy-done.1), custom_call_target="tpu_custom_call" | custom-call | tf_op jit(solution)/shard_map/meet/pallas_call | solution.py:390
  165.3 1.2 collective-permute-start.2
  166.4 3.9 %collective-permute-done.2 = f32[4,2,32,64]{3,2,1,0:T(8,128)S(1)} collective-permute-done((f32[4,2,32,64]{3,2,1,0:T(8,128)S(1)}, f32[4,2,32,64]{3,2,1,0:T(8,128)S(1)}, u32[]{:S(2)}, u32[]{:S(2)}) %collective-permute-start.2) | collective-permute-done | bytes 65568 | tf_op jit(solution)/shard_map/ppermute | solution.py:438
  170.4 5.5 %collective-permute-start.3 = (f32[2,2,32,64]{3,2,1,0:T(8,128)S(1)}, f32[2,2,32,64]{3,2,1,0:T(8,128)S(1)}, u32[]{:S(2)}, u32[]{:S(2)}) collective-permute-start(f32[2,2,32,64]{3,2,1,0:T(8,128)S(1)} %slice.62), channel_id=1, source_target_pairs={{8,0},{10,2},{12,4},{14,6},{16,8},{18,10},{20,12},{22,14},{24,16},... | collective-permute-start | bytes 98312 | tf_op jit(solution)/shard_map/ppermute | solution.py:439
  175.8 26.5 %collective-permute-done.3 = f32[2,2,32,64]{3,2,1,0:T(8,128)S(1)} collective-permute-done((f32[2,2,32,64]{3,2,1,0:T(8,128)S(1)}, f32[2,2,32,64]{3,2,1,0:T(8,128)S(1)}, u32[]{:S(2)}, u32[]{:S(2)}) %collective-permute-start.3) | collective-permute-done | bytes 32800 | tf_op jit(solution)/shard_map/ppermute | solution.py:439
  202.3 8.5 %collective-permute-start.4 = (f32[2,32,64]{2,1,0:T(8,128)S(1)}, f32[2,32,64]{2,1,0:T(8,128)S(1)}, u32[]{:S(2)}, u32[]{:S(2)}) collective-permute-start(f32[2,32,64]{2,1,0:T(8,128)S(1)} %get-tuple-element.17), channel_id=1, source_target_pairs={{24,0},{26,2},{28,4},{30,6},{0,8},{2,10},{4,12},{6,14},{8,16},{10,... | collective-permute-start | bytes 49160 | tf_op jit(solution)/shard_map/ppermute | solution.py:440
  210.8 2.5 %collective-permute-done.4 = f32[2,32,64]{2,1,0:T(8,128)S(1)} collective-permute-done((f32[2,32,64]{2,1,0:T(8,128)S(1)}, f32[2,32,64]{2,1,0:T(8,128)S(1)}, u32[]{:S(2)}, u32[]{:S(2)}) %collective-permute-start.4) | collective-permute-done | bytes 16416 | tf_op jit(solution)/shard_map/ppermute | solution.py:440
  213.2 0.7 select_select_fusion
  (6 shorter events, 0.1 us)
Async XLA Ops:
  2.7 12.4 %collective-permute-start.1 = (s32[2]{0:T(128)S(1)}, s32[2]{0:T(128)S(1)}, u32[]{:S(2)}, u32[]{:S(2)}) collective-permute-start(s32[2]{0:T(128)S(1)} %pad_add_fusion.1), channel_id=1, source_target_pairs={{8,0},{10,2},{12,4},{14,6},{16,8},{18,10},{20,12},{22,14},{24,16},... | collective-permute-start | bytes 32 | tf_op jit(solution)/shard_map/ppermute | solution.py:424
  7.8 5.4 %collective-permute-start = (s32[2]{0:T(128)S(1)}, s32[2]{0:T(128)S(1)}, u32[]{:S(2)}, u32[]{:S(2)}) collective-permute-start(s32[2]{0:T(128)S(1)} %pad_add_fusion.1), channel_id=1, source_target_pairs={{24,0},{26,2},{28,4},{30,6},{0,8},{2,10},{4,12},{6,14},{8,16},{10,... | collective-permute-start | bytes 32 | tf_op jit(solution)/shard_map/ppermute | solution.py:423
  27.1 4.9 %copy-start.2 = (s32[2,4,108]{2,1,0:T(4,128)S(1)}, s32[2,4,108]{2,1,0:T(4,128)}, u32[]{:S(2)}) copy-start(s32[2,4,108]{2,1,0:T(4,128)} %get-tuple-element.8.local_ref) | copy-start | bytes 10372
  32.1 2.1 copy-start
  34.2 1.3 copy-start.1
  165.3 5.0 %collective-permute-start.2 = (f32[4,2,32,64]{3,2,1,0:T(8,128)S(1)}, f32[4,2,32,64]{3,2,1,0:T(8,128)S(1)}, u32[]{:S(2)}, u32[]{:S(2)}) collective-permute-start(f32[4,2,32,64]{3,2,1,0:T(8,128)S(1)} %slice_select_fusion), channel_id=1, source_target_pairs={{0,1},{1,0},{2,3},{3,2},{4,5},{5,4},{6,7},{7,6},{8,9},{9,8},{10,11... | collective-permute-start | bytes 196616 | tf_op jit(solution)/shard_map/ppermute | solution.py:438
  170.4 31.9 %collective-permute-start.3 = (f32[2,2,32,64]{3,2,1,0:T(8,128)S(1)}, f32[2,2,32,64]{3,2,1,0:T(8,128)S(1)}, u32[]{:S(2)}, u32[]{:S(2)}) collective-permute-start(f32[2,2,32,64]{3,2,1,0:T(8,128)S(1)} %slice.62), channel_id=1, source_target_pairs={{8,0},{10,2},{12,4},{14,6},{16,8},{18,10},{20,12},{22,14},{24,16},... | collective-permute-start | bytes 98312 | tf_op jit(solution)/shard_map/ppermute | solution.py:439
  202.3 10.9 %collective-permute-start.4 = (f32[2,32,64]{2,1,0:T(8,128)S(1)}, f32[2,32,64]{2,1,0:T(8,128)S(1)}, u32[]{:S(2)}, u32[]{:S(2)}) collective-permute-start(f32[2,32,64]{2,1,0:T(8,128)S(1)} %get-tuple-element.17), channel_id=1, source_target_pairs={{24,0},{26,2},{28,4},{30,6},{0,8},{2,10},{4,12},{6,14},{8,16},{10,... | collective-permute-start | bytes 49160 | tf_op jit(solution)/shard_map/ppermute | solution.py:440

commit v4 on v3

--- a/solution.py
+++ b/solution.py
@@ -252,15 +252,25 @@
     swap_own.start()
     for c in range(CHUNKS):
 
+        @pl.when(even & rises)
+        def _():
+            rise[c].start()
+
+        @pl.when(~even & falls)
+        def _():
+            fall[c].start()
+
+    for c in range(CHUNKS):
+
         @pl.when(column > 0)
         def _():
             pass_own[c].start()
 
-        @pl.when(falls)
+        @pl.when(even)
         def _():
             fall[c].start()
 
-        @pl.when(rises)
+        @pl.when(~even)
         def _():
             rise[c].start()
 

time: 214 us -> 196 us (0.916)
  waiting for transfers between devices: 38.1 us -> 17.2 us
    ppermute x1, waiting for transfers between devices: 26.5 us -> 1.91 us  [on_four_rows(): from_upper = lax.ppermute(total[1:3], 'ka', to_lower)]
    ppermute x1, starting transfers between devices: 5.46 us -> 15.9 us  [on_four_rows(): from_upper = lax.ppermute(total[1:3], 'ka', to_lower)]
    ppermute x1, starting transfers between devices: 8.45 us -> 0.06 us  [on_four_rows(): from_lower = lax.ppermute(total[3], 'ka', to_upper)]
    ppermute x1, waiting for transfers between devices: 2.45 us -> 6.04 us  [on_four_rows(): from_lower = lax.ppermute(total[3], 'ka', to_upper)]
where the time goes in v4:
time: 196 us; the launch traced here: 195 us
  Pallas kernels  142 us (72%)
  starting transfers between devices  22.2 us (11%)
  waiting for transfers between devices  17.2 us (9%)
  other arithmetic  6.92 us (4%)
  local copies, waits for them, and re-layouts  5.42 us (3%)
    pallas_call x1, Pallas kernels, meet(): pl.pallas_call(functools.partial(meet_kernel, points, slab, capacity), ou...  130 us
    ppermute x1, starting transfers between devices, on_four_rows(): from_upper = lax.ppermute(total[1:3], 'ka', to_lower)  15.9 us
    pallas_call x1, Pallas kernels, plan(): pl.pallas_call(functools.partial(plan_kernel, slab, capacity), out_shape=...  8.9 us
    ppermute x1, waiting for transfers between devices, on_four_rows(): from_lower = lax.ppermute(total[3], 'ka', to_upper)  6.04 us
    ppermute x1, waiting for transfers between devices, on_four_rows(): lower = lax.ppermute(sent, 'ka', to_upper)  5.28 us
    ppermute x1, starting transfers between devices, on_four_rows(): upper = lax.ppermute(sent, 'ka', to_lower)  5.08 us
    ppermute x1, waiting for transfers between devices, on_four_rows(): lax.ppermute(jnp.where(first, high_rows, low_rows), 'ga', swap)  3.94 us
  transfers between devices with their start and end apart: 5, of which 4 were waited for; matrix products, arithmetic and copies ran while one was open for 0% of the time, Pallas kernels for 0%

profile of v4, /device:TPU:0, one launch (start us, length us, event | category | flops | bytes accessed | tf_op | source)
XLA Modules:
  0.0 195.0 jit_solution(17366008245291745012)
XLA Ops:
  0.0 1.4 fusion.3
  1.4 1.3 pad_add_fusion.1
  2.7 5.1 %collective-permute-start.1 = (s32[2]{0:T(128)S(1)}, s32[2]{0:T(128)S(1)}, u32[]{:S(2)}, u32[]{:S(2)}) collective-permute-start(s32[2]{0:T(128)S(1)} %pad_add_fusion.1), channel_id=1, source_target_pairs={{8,0},{10,2},{12,4},{14,6},{16,8},{18,10},{20,12},{22,14},{24,16},... | collective-permute-start | bytes 32 | tf_op jit(solution)/shard_map/ppermute | solution.py:434
  7.8 0.0 collective-permute-start
  7.8 0.1 pad_add_fusion
  7.9 5.3 %collective-permute-done = s32[2]{0:T(128)S(1)} collective-permute-done((s32[2]{0:T(128)S(1)}, s32[2]{0:T(128)S(1)}, u32[]{:S(2)}, u32[]{:S(2)}) %collective-permute-start) | collective-permute-done | bytes 40 | tf_op jit(solution)/shard_map/ppermute | solution.py:433
  13.2 0.7 fusion.6
  15.1 0.0 collective-permute-done.1
  15.1 0.6 slice.47
  15.7 2.5 %pad_add_fusion.2.shift_ref = s32[4]{0:T(128)} fusion(s32[1]{0:T(128)} %slice.47, s32[1]{0:T(128)} %get-tuple-element.24, s32[1]{0:T(128)} %bitcast.8, s32[1]{0:T(128)} %bitcast.2), kind=kLoop, calls=%fused_computation.17 | loop fusion | flops 12 | bytes 32 | tf_op jit(solution)/shard_map/stack | solution.py:435
  18.2 8.9 %plan.1 = (s32[2,4,108]{2,1,0:T(4,128)}, s32[4,28]{1,0:T(4,128)}, s32[4,28]{1,0:T(4,128)}) custom-call(s32[4]{0:T(128)} %pad_add_fusion.2.shift_ref, s32[8,240]{1,0:T(8,128)} %map_ref.1), custom_call_target="tpu_custom_call" | custom-call | tf_op jit(solution)/shard_map/plan/pallas_call | solution.py:191
  27.1 0.0 copy-start.2
  27.2 0.8 slice_select_fusion.2
  27.9 0.7 reshape.36.index_ref
  28.6 0.1 reshape.35.send_ref
  28.7 3.4 %gather_blocks.1.mine_out = bf16[40,2,64,128]{3,2,1,0:T(8,128)(2,1)} custom-call(s32[40]{0:T(128)} %reshape.36.index_ref, bf16[120,2,64,128]{3,2,1,0:T(8,128)(2,1)} %bitcast.35), custom_call_target="tpu_custom_call" | custom-call | bytes 5242880 | tf_op jit(solution)/shard_map/gather_blocks/pallas_call | solution.py:150
  32.0 0.0 copy-done.2
  32.1 0.0 copy-start
  32.1 2.1 %copy-done = bf16[1,120,2,64,128]{4,3,2,1,0:T(8,128)(2,1)S(1)} copy-done((bf16[1,120,2,64,128]{4,3,2,1,0:T(8,128)(2,1)S(1)}, bf16[1,120,2,64,128]{4,3,2,1,0:T(8,128)(2,1)}, u32[]{:S(2)}) %copy-start) | copy-done | bytes 3932184
  34.2 0.0 copy-start.1
  34.2 1.3 copy-done.1
  35.5 129.7 %meet.1 = f32[4,2,64,64]{3,2,1,0:T(8,128)S(1)} custom-call(s32[2,4,108]{2,1,0:T(4,128)S(1)} %copy-done.2, s32[4,20]{1,0:T(4,128)S(1)} %get-tuple-element.20.other_ref, s32[40]{0:T(128)S(1)} %reshape.35.send_ref, bf16[120,2,64,128]{3,2,1,0:T(8,128)(2,1)S(1)} %bitcast.36, bf16[40,2,64,128]{3,2,1,0:T(8,128)(2,1)S(1)} %copy-done.1), custom_call_target="tpu_custom_call" | custom-call | tf_op jit(solution)/shard_map/meet/pallas_call | solution.py:400
  165.2 1.1 collective-permute-start.2
  166.3 3.9 %collective-permute-done.2 = f32[4,2,32,64]{3,2,1,0:T(8,128)S(1)} collective-permute-done((f32[4,2,32,64]{3,2,1,0:T(8,128)S(1)}, f32[4,2,32,64]{3,2,1,0:T(8,128)S(1)}, u32[]{:S(2)}, u32[]{:S(2)}) %collective-permute-start.2) | collective-permute-done | bytes 65568 | tf_op jit(solution)/shard_map/ppermute | solution.py:448
  170.3 15.9 %collective-permute-start.3 = (f32[2,2,32,64]{3,2,1,0:T(8,128)S(1)}, f32[2,2,32,64]{3,2,1,0:T(8,128)S(1)}, u32[]{:S(2)}, u32[]{:S(2)}) collective-permute-start(f32[2,2,32,64]{3,2,1,0:T(8,128)S(1)} %slice.62), channel_id=1, source_target_pairs={{8,0},{10,2},{12,4},{14,6},{16,8},{18,10},{20,12},{22,14},{24,16},... | collective-permute-start | bytes 98312 | tf_op jit(solution)/shard_map/ppermute | solution.py:449
  186.3 1.9 collective-permute-done.3
  188.2 0.1 collective-permute-start.4
  188.2 6.0 %collective-permute-done.4 = f32[2,32,64]{2,1,0:T(8,128)S(1)} collective-permute-done((f32[2,32,64]{2,1,0:T(8,128)S(1)}, f32[2,32,64]{2,1,0:T(8,128)S(1)}, u32[]{:S(2)}, u32[]{:S(2)}) %collective-permute-start.4) | collective-permute-done | bytes 16416 | tf_op jit(solution)/shard_map/ppermute | solution.py:450
  194.3 0.7 select_select_fusion
  (6 shorter events, 0.1 us)
Async XLA Ops:
  2.7 12.4 %collective-permute-start.1 = (s32[2]{0:T(128)S(1)}, s32[2]{0:T(128)S(1)}, u32[]{:S(2)}, u32[]{:S(2)}) collective-permute-start(s32[2]{0:T(128)S(1)} %pad_add_fusion.1), channel_id=1, source_target_pairs={{8,0},{10,2},{12,4},{14,6},{16,8},{18,10},{20,12},{22,14},{24,16},... | collective-permute-start | bytes 32 | tf_op jit(solution)/shard_map/ppermute | solution.py:434
  7.8 5.4 %collective-permute-start = (s32[2]{0:T(128)S(1)}, s32[2]{0:T(128)S(1)}, u32[]{:S(2)}, u32[]{:S(2)}) collective-permute-start(s32[2]{0:T(128)S(1)} %pad_add_fusion.1), channel_id=1, source_target_pairs={{24,0},{26,2},{28,4},{30,6},{0,8},{2,10},{4,12},{6,14},{8,16},{10,... | collective-permute-start | bytes 32 | tf_op jit(solution)/shard_map/ppermute | solution.py:433
  27.1 4.9 %copy-start.2 = (s32[2,4,108]{2,1,0:T(4,128)S(1)}, s32[2,4,108]{2,1,0:T(4,128)}, u32[]{:S(2)}) copy-start(s32[2,4,108]{2,1,0:T(4,128)} %get-tuple-element.8.local_ref) | copy-start | bytes 10372
  32.1 2.1 %copy-start = (bf16[1,120,2,64,128]{4,3,2,1,0:T(8,128)(2,1)S(1)}, bf16[1,120,2,64,128]{4,3,2,1,0:T(8,128)(2,1)}, u32[]{:S(2)}) copy-start(bf16[1,120,2,64,128]{4,3,2,1,0:T(8,128)(2,1)} %param.4) | copy-start | bytes 11796484
  34.2 1.3 copy-start.1
  165.2 5.0 %collective-permute-start.2 = (f32[4,2,32,64]{3,2,1,0:T(8,128)S(1)}, f32[4,2,32,64]{3,2,1,0:T(8,128)S(1)}, u32[]{:S(2)}, u32[]{:S(2)}) collective-permute-start(f32[4,2,32,64]{3,2,1,0:T(8,128)S(1)} %slice_select_fusion), channel_id=1, source_target_pairs={{0,1},{1,0},{2,3},{3,2},{4,5},{5,4},{6,7},{7,6},{8,9},{9,8},{10,11... | collective-permute-start | bytes 196616 | tf_op jit(solution)/shard_map/ppermute | solution.py:448
  170.3 17.8 %collective-permute-start.3 = (f32[2,2,32,64]{3,2,1,0:T(8,128)S(1)}, f32[2,2,32,64]{3,2,1,0:T(8,128)S(1)}, u32[]{:S(2)}, u32[]{:S(2)}) collective-permute-start(f32[2,2,32,64]{3,2,1,0:T(8,128)S(1)} %slice.62), channel_id=1, source_target_pairs={{8,0},{10,2},{12,4},{14,6},{16,8},{18,10},{20,12},{22,14},{24,16},... | collective-permute-start | bytes 98312 | tf_op jit(solution)/shard_map/ppermute | solution.py:449
  188.2 6.1 %collective-permute-start.4 = (f32[2,32,64]{2,1,0:T(8,128)S(1)}, f32[2,32,64]{2,1,0:T(8,128)S(1)}, u32[]{:S(2)}, u32[]{:S(2)}) collective-permute-start(f32[2,32,64]{2,1,0:T(8,128)S(1)} %get-tuple-element.17), channel_id=1, source_target_pairs={{24,0},{26,2},{28,4},{30,6},{0,8},{2,10},{4,12},{6,14},{8,16},{10,... | collective-permute-start | bytes 49160 | tf_op jit(solution)/shard_map/ppermute | solution.py:450
